TPU v7x, 256 devices: a whole 4x4x8 slice. The times are simulated.
256 devices in a mesh: lon: 32 (over x_lo, z, core), lat: 8 (over x_hi, y).
Axes of the slice: x: 4 (x_hi: 2, x_lo: 2; x = x_hi * 2 + x_lo), y: 4, z: 8, core: 2. Of those that a mesh axis runs over, the one named last changes fastest.
Arguments:
- zonal_state: float32 [4, 32, 3, 32, 4096], P(None, None, None, 'lat', 'lon'), may hold values from -6 to 6
- zonal_courant: float32 [32, 32, 4096], P(None, 'lat', 'lon'), may hold values from -0.5 to 0.5
- zonal_length: int32 [32], P('lat'), may hold values from 1024 to 4096, as said below
- zonal_owner: int32 [32, 4096], P('lat', 'lon'), may hold values from 0 to 127, as said below
- merid_state: float32 [4, 32, 3, 128, 1024], P(None, None, None, 'lon', 'lat'), may hold values from -6 to 6
- merid_courant: float32 [32, 128, 1024], P(None, 'lon', 'lat'), may hold values from -0.5 to 0.5
- mixing: float32 [4, 32, 32], replicated, may hold values from -0.18 to 0.18
Outputs:
- zonal_next: float32 [4, 32, 3, 32, 4096], P(None, None, None, 'lat', 'lon')
- merid_next: float32 [4, 32, 3, 128, 1024], P(None, None, None, 'lon', 'lat')
- coupling: float32 [128, 32, 128], P('lon', 'lat')
Inputs may be any that keep to these rules, and one draw needn't show every extreme that they name: `zonal_owner`: non-decreasing along each row; each GCM column holds 16 to 48 consecutive cells of a row, and cell x belongs to a column g with |g - x // 32| <= 1. `zonal_length`: in each latitude sector (aligned blocks of 4 cycles) the first cycle holds 2112 cells and the second 4096.
All inputs are finite; a program needn't handle non-finite values.
Results may differ from a plain program's by a relative error of at most 0.0003.
Values sent between devices are 32-bit elements; how exact they have to be, the bound alone decides.
A program may use at most 64 MiB of HBM per device.

v0:
```python
import functools

import jax
import jax.numpy as jnp
from jax import lax
from jax.experimental import pallas as pl
from jax.experimental.pallas import tpu as pltpu
from jax.sharding import PartitionSpec as P

SUB = 4
OFF = 8
CELLS = 128
LANES = 128
ROWS = 152
WIN = 16
SROWS = 32
PROWS = 272
PBASE = 136
GLON_DEV = 4
FAR = (0, 2, 3)
MESH = pl.DeviceIdType.MESH
F32 = jnp.float32
BF16 = jnp.bfloat16


def two_parts(value):
    high = value.astype(BF16)
    low = (value - high.astype(F32)).astype(BF16)
    return high, low


def advance(src, dst, courant, weights, lhs, products, items, rows, chunk, ahead):
    for n, item in enumerate(items):
        for w in range(3):
            for at in range(0, rows, chunk):
                high, low = two_parts(src(item, w, OFF + at, chunk))
                spot = pl.ds((n * 3 + w) * rows + at, chunk)
                lhs[spot, 0:LANES] = high
                lhs[spot, LANES:] = low
    total = len(items) * 3 * rows
    for at in range(0, total, ahead):
        size = min(ahead, total - at)
        products[pl.ds(at, size), :] = jnp.dot(
            lhs[pl.ds(at, size), :], weights[...], preferred_element_type=F32
        )
    for n, item in enumerate(items):
        for at in range(0, rows, chunk):
            half = 0.5 * courant(item, at, chunk)
            ahead_share, behind_share = 0.3 - half, 0.3 + half
            now = [src(item, w, OFF + at, chunk) for w in range(3)]
            for w, (one, other) in enumerate(((0, 1), (0, 2), (1, 2))):
                spot = pl.ds((n * 3 + w) * rows + at, chunk)
                mixed = products[spot, 0:LANES] + products[spot, LANES:]
                along = ahead_share * src(item, w, OFF + at + 1, chunk) + behind_share * src(
                    item, w, OFF + at - 1, chunk
                )
                dst(item, w, OFF + at, chunk, mixed + along + 0.1 * (now[one] + now[other]))


def kernel(
    counts,
    zlen,
    zs,
    zc,
    owner,
    ms,
    mc,
    mix,
    out_z,
    out_m,
    out_c,
    raw,
    rawc,
    first,
    state,
    weights,
    lhs,
    products,
    strips,
    scour,
    slhs,
    sproducts,
    back,
    edges,
    halos,
    tails,
    gathered,
    gathered_0,
    heads,
    part,
    part_in,
    load_sem,
    send_sem,
    recv_sem,
    far_send,
    far_recv,
):
    lon_count, lat_count = counts
    half_turn = lon_count // 2
    tail_from = lon_count // 4 - 1
    tail_devs = list(range(tail_from, lon_count))
    me, lat = lax.axis_index("lon"), lax.axis_index("lat")
    left = lax.rem(me + lon_count - 1, lon_count)
    right = lax.rem(me + 1, lon_count)
    across = lax.rem(me + half_turn, lon_count)
    at_south, at_north = lat == 0, lat == lat_count - 1
    south = {"lon": jnp.where(at_south, across, me), "lat": jnp.where(at_south, lat, lat - 1)}
    north = {"lon": jnp.where(at_north, across, me), "lat": jnp.where(at_north, lat, lat + 1)}
    west, east = {"lon": left, "lat": lat}, {"lon": right, "lat": lat}
    root = {"lon": 0 * me, "lat": lat}
    is_root, is_tail, is_half = me == 0, me >= tail_from, me == half_turn

    barrier = pltpu.get_barrier_semaphore()
    for peer in (west, east, south, north):
        pl.semaphore_signal(barrier, inc=1, device_id=peer, device_id_type=MESH)

    @pl.when(is_tail)
    def _():
        pl.semaphore_signal(barrier, inc=1, device_id=root, device_id_type=MESH)

    @pl.when(is_root)
    def _():
        for dev in tail_devs:
            pl.semaphore_signal(
                barrier, inc=1, device_id={"lon": 0 * me + dev, "lat": lat}, device_id_type=MESH
            )

    loads = []
    for f, (s_ref, c_ref) in enumerate(((zs, zc), (ms, mc))):
        loads.append(pltpu.make_async_copy(s_ref, raw.at[f], load_sem.at[f, 0]))
        loads.append(pltpu.make_async_copy(c_ref, rawc.at[f], load_sem.at[f, 1]))
    for load in loads:
        load.start()

    spread = jnp.concatenate([mix[...]] * 4, axis=1)
    row_at = lax.broadcasted_iota(jnp.int32, (LANES, LANES), 0)
    lane_at = lax.broadcasted_iota(jnp.int32, (LANES, LANES), 1)
    spread = jnp.where(row_at // 32 == lane_at // 32, spread, 0.0)
    spread = spread + jnp.where(row_at == lane_at, 0.2, 0.0)
    high, low = two_parts(spread.T)
    for row in (0, LANES):
        weights[row : row + LANES, 0:LANES] = high
        weights[row : row + LANES, LANES:] = low

    def turn_in(f):
        loads[2 * f].wait()
        loads[2 * f + 1].wait()
        for r in range(4):
            for w in range(3):
                turned = raw[f, pl.ds(w * 4 + r, LANES, stride=12), :].T
                first[4 * f + r, w, OFF : OFF + CELLS, :] = turned
                state[0, 4 * f + r, w, OFF : OFF + CELLS, :] = turned
            c_now = rawc[f, pl.ds(r, 32, stride=4), :]
            first[4 * f + r, 3, OFF : OFF + CELLS, :] = jnp.concatenate([c_now] * 4, axis=0).T
        for r in range(4):
            for p in range(4):
                edges[f, 0, r, 4 * p : 4 * p + 4, :] = first[4 * f + r, p, OFF : OFF + SUB, :]
                edges[f, 1, r, 4 * p : 4 * p + 4, :] = first[
                    4 * f + r, p, OFF + CELLS - SUB : OFF + CELLS, :
                ]

    turn_in(0)
    ends = [jnp.clip(zlen[r] - me * CELLS, 0, CELLS + SUB) for r in range(4)]
    quarter = lax.broadcasted_iota(jnp.int32, (8, LANES), 0)
    for r in FAR:
        cell = ends[r] - SUB + quarter
        own = (cell >= 0) & (cell < CELLS)
        for p in range(4):
            found = jnp.where(own, first[r, p, pl.ds(OFF + ends[r] - SUB, 8), :], 0.0)
            tails[r, 4 * p : 4 * p + 4, :] = found[0:SUB]
    turn_in(1)

    def interior(f):
        def step(t, carry):
            now, then = lax.rem(t, 2), lax.rem(t + 1, 2)

            def src(ch, w, at, size):
                return state[now, ch, w, pl.ds(at, size), :]

            def dst(ch, w, at, size, value):
                state[then, ch, w, pl.ds(at, size), :] = value

            advance(
                src,
                dst,
                lambda ch, at, size: first[ch, 3, pl.ds(OFF + at, size), :],
                weights,
                lhs,
                products,
                [4 * f + r for r in range(4)],
                CELLS,
                32,
                384,
            )
            return carry

        lax.fori_loop(0, SUB, step, 0)

    interior(0)

    peers = 4 + jnp.where(is_tail, 1, 0) + jnp.where(is_root, len(tail_devs), 0)
    pl.semaphore_wait(barrier, peers)

    def remote(src, dst, s_sem, r_sem, peer):
        return pltpu.make_async_remote_copy(
            src_ref=src,
            dst_ref=dst,
            send_sem=s_sem,
            recv_sem=r_sem,
            device_id=peer,
            device_id_type=MESH,
        )

    slot = jnp.maximum(me - tail_from, 0)
    tail_copy = remote(
        tails.at[2:4], gathered.at[slot], far_send.at[0], far_recv.at[slot], root
    )
    tail_0_copy = remote(
        tails.at[0], gathered_0, far_send.at[1], recv_sem.at[7], root
    )
    head_copies = [
        remote(
            edges.at[0, 0, 2:4],
            heads.at[2:4],
            far_send.at[2 + n],
            recv_sem.at[8],
            {"lon": 0 * me + dev, "lat": lat},
        )
        for n, dev in enumerate(tail_devs)
    ]
    head_0_copy = remote(
        edges.at[0, 0, 0],
        heads.at[0],
        far_send.at[2 + len(tail_devs)],
        recv_sem.at[9],
        {"lon": 0 * me + half_turn, "lat": lat},
    )

    @pl.when(is_tail)
    def _():
        tail_copy.start()

    @pl.when(is_half)
    def _():
        tail_0_copy.start()

    @pl.when(is_root)
    def _():
        head_0_copy.start()
        for copy in head_copies:
            copy.start()

    south_side, north_side = jnp.where(at_south, 0, 1), jnp.where(at_north, 1, 0)
    near = [
        remote(edges.at[0, 0], halos.at[0, 1], send_sem.at[0], recv_sem.at[1], west),
        remote(edges.at[0, 1], halos.at[0, 0], send_sem.at[1], recv_sem.at[0], east),
        remote(
            edges.at[1, 0],
            halos.at[1, south_side],
            send_sem.at[2],
            recv_sem.at[2 + south_side],
            south,
        ),
        remote(
            edges.at[1, 1],
            halos.at[1, north_side],
            send_sem.at[3],
            recv_sem.at[2 + north_side],
            north,
        ),
    ]
    for copy in near:
        copy.start()

    interior(1)

    def arrived(f, side):
        pltpu.make_async_copy(
            halos.at[f, side], halos.at[f, side], recv_sem.at[2 * f + side]
        ).wait()

    def strip_src(now):
        return lambda n, w, at, size: strips[now, n, w, pl.ds(at, size), :]

    def strip_steps(count):
        def step(t, carry):
            now, then = lax.rem(t, 2), lax.rem(t + 1, 2)

            def dst(n, w, at, size, value):
                strips[then, n, w, pl.ds(at, size), :] = value

            advance(
                strip_src(now),
                dst,
                lambda n, at, size: scour[n, pl.ds(at, size), :],
                weights,
                slhs,
                sproducts,
                list(range(count)),
                WIN,
                16,
                count * 3 * WIN,
            )
            return carry

        lax.fori_loop(0, SUB, step, 0)

    def fill(n, ch, start):
        for w in range(3):
            strips[0, n, w, OFF : OFF + WIN, :] = first[ch, w, pl.ds(start, WIN), :]
        scour[n, :, :] = first[ch, 3, pl.ds(start, WIN), :]

    left_row, right_row = OFF - SUB, OFF + CELLS
    for f, side in ((0, 0), (0, 1), (1, 0), (1, 1)):
        arrived(f, side)
    for r in range(4):
        for p in range(4):
            first[r, p, right_row : right_row + SUB, :] = halos[0, 1, r, 4 * p : 4 * p + 4, :]
    for side, turned, row in ((0, at_south, left_row), (1, at_north, right_row)):
        for r in range(4):
            for p in range(4):
                plain = halos[1, side, r, 4 * p : 4 * p + 4, :]
                q = p if p == 3 else 2 - p
                mirrored = jnp.concatenate(
                    [halos[1, side, r, 4 * q + 3 - j : 4 * q + 4 - j, :] for j in range(SUB)],
                    axis=0,
                )
                if p == 3:
                    mirrored = -mirrored
                first[4 + r, p, row : row + SUB, :] = jnp.where(turned, mirrored, plain)
    left_start, right_start = OFF - SUB, OFF + CELLS + SUB - WIN
    for r in range(4):
        fill(r, r, right_start)
        fill(4 + r, 4 + r, left_start)
        fill(8 + r, 4 + r, right_start)
    strip_steps(12)
    for r in range(4):
        for w in range(3):
            kept = strips[0, r, w, OFF + 8 : OFF + 12, :]
            state[0, r, w, OFF + CELLS - SUB : OFF + CELLS, :] = kept
            kept = strips[0, 4 + r, w, OFF + 4 : OFF + 8, :]
            state[0, 4 + r, w, OFF : OFF + SUB, :] = kept
            kept = strips[0, 8 + r, w, OFF + 8 : OFF + 12, :]
            state[0, 4 + r, w, OFF + CELLS - SUB : OFF + CELLS, :] = kept
    for r in range(4):
        for w in range(3):
            out_m[pl.ds(w * 4 + r, LANES, stride=12), :] = state[
                0, 4 + r, w, OFF : OFF + CELLS, :
            ].T

    @pl.when(is_root)
    def _():
        for n in range(len(tail_devs)):
            pltpu.make_async_copy(gathered.at[n], gathered.at[n], far_recv.at[n]).wait()
        pltpu.make_async_copy(gathered_0, gathered_0, recv_sem.at[7]).wait()

    @pl.when(is_tail)
    def _():
        pltpu.make_async_copy(heads.at[2:4], heads.at[2:4], recv_sem.at[8]).wait()

    @pl.when(is_half)
    def _():
        pltpu.make_async_copy(heads.at[0], heads.at[0], recv_sem.at[9]).wait()

    for r in range(4):
        if r == 1:
            tail_cells = None
        elif r == 0:
            tail_cells = gathered_0[...]
        else:
            tail_cells = gathered[0, r - 2]
            for n in range(1, len(tail_devs)):
                tail_cells = tail_cells + gathered[n, r - 2]
        for p in range(4):
            plain = halos[0, 0, r, 4 * p : 4 * p + 4, :]
            if tail_cells is not None:
                plain = jnp.where(is_root, tail_cells[4 * p : 4 * p + 4], plain)
            first[r, p, left_row : left_row + SUB, :] = plain
    for r in range(4):
        fill(r, r, left_start)
    for n, r in enumerate(FAR):
        fill(4 + n, r, ends[r])
        for w in range(3):
            strips[0, 4 + n, w, OFF + 8 : OFF + 12, :] = heads[r, 4 * w : 4 * w + 4, :]
        scour[4 + n, 8:12, :] = heads[r, 12:16, :]
    strip_steps(7)
    for r in range(4):
        for w in range(3):
            kept = strips[0, r, w, OFF + 4 : OFF + 8, :]
            state[0, r, w, OFF : OFF + SUB, :] = kept
    for n, r in enumerate(FAR):
        for w in range(3):
            back[n, w, PBASE : PBASE + WIN, :] = strips[0, 4 + n, w, OFF : OFF + WIN, :]

    near_columns = me * GLON_DEV - 1 + lax.broadcasted_iota(jnp.int32, (8, CELLS), 0)
    column = lax.broadcasted_iota(jnp.int32, (CELLS, LANES), 0)
    scale = GLON_DEV / (3.0 * CELLS)
    for r in range(4):
        change = None
        for w in range(3):
            value = state[0, r, w, OFF : OFF + CELLS, :]
            before = first[r, w, OFF : OFF + CELLS, :]
            if r in FAR:
                n = FAR.index(r)
                cut = ends[r]
                strip = back[n, w, pl.ds(PBASE + 8 - cut, CELLS), :]
                value = jnp.where(column >= cut - SUB, strip, value)
                value = jnp.where(column < cut, value, before)
            out_z[pl.ds(w * 4 + r, LANES, stride=12), :] = value.T
            change = value - before if change is None else change + (value - before)
        high, low = two_parts(change * scale)
        mine = (jnp.broadcast_to(owner[r : r + 1, :], (8, CELLS)) == near_columns).astype(BF16)
        part[r, :, :] = jnp.dot(
            jnp.concatenate([mine, mine], axis=1),
            jnp.concatenate([high, low], axis=0),
            preferred_element_type=F32,
        )
    for r in range(4):
        part[4, r : r + 1, :] = part[r, 0:1, :]
        part[5, r : r + 1, :] = part[r, 5:6, :]
    back_copy = remote(part.at[4], part_in.at[1], send_sem.at[4], recv_sem.at[5], west)
    on_copy = remote(part.at[5], part_in.at[0], send_sem.at[5], recv_sem.at[4], east)
    back_copy.start()
    on_copy.start()
    back_copy.wait_recv()
    on_copy.wait_recv()
    for r in range(4):
        for g in range(GLON_DEV):
            value = part[r, g + 1 : g + 2, :]
            if g == 0:
                value = value + part_in[0, r : r + 1, :]
            if g == GLON_DEV - 1:
                value = value + part_in[1, r : r + 1, :]
            out_c[4 * g + r : 4 * g + r + 1, :] = value

    for copy in near:
        copy.wait_send()
    back_copy.wait_send()
    on_copy.wait_send()

    @pl.when(is_tail)
    def _():
        tail_copy.wait_send()

    @pl.when(is_half)
    def _():
        tail_0_copy.wait_send()

    @pl.when(is_root)
    def _():
        head_0_copy.wait_send()
        for copy in head_copies:
            copy.wait_send()


def shards(
    counts, zonal_state, zonal_courant, zonal_length, zonal_owner, merid_state, merid_courant, mixing
):
    tail_count = counts[0] - (counts[0] // 4 - 1)
    hbm = pl.BlockSpec(memory_space=pltpu.HBM)
    vmem = pl.BlockSpec(memory_space=pltpu.VMEM)
    smem = pl.BlockSpec(memory_space=pltpu.SMEM)
    flat_shape = (LANES * 12, CELLS)
    out_z, out_m, out_c = pl.pallas_call(
        functools.partial(kernel, counts),
        out_shape=(
            jax.ShapeDtypeStruct(flat_shape, F32),
            jax.ShapeDtypeStruct(flat_shape, F32),
            jax.ShapeDtypeStruct((4 * GLON_DEV, LANES), F32),
        ),
        in_specs=[smem, hbm, hbm, vmem, hbm, hbm, vmem],
        out_specs=(vmem, vmem, vmem),
        scratch_shapes=[
            pltpu.VMEM((2, *flat_shape), F32),
            pltpu.VMEM((2, LANES, CELLS), F32),
            pltpu.VMEM((8, 4, ROWS, LANES), F32),
            pltpu.VMEM((2, 8, 3, ROWS, LANES), F32),
            pltpu.VMEM((2 * LANES, 2 * LANES), BF16),
            pltpu.VMEM((4 * 3 * CELLS, 2 * LANES), BF16),
            pltpu.VMEM((4 * 3 * CELLS, 2 * LANES), F32),
            pltpu.VMEM((2, 12, 3, SROWS, LANES), F32),
            pltpu.VMEM((12, WIN, LANES), F32),
            pltpu.VMEM((12 * 3 * WIN, 2 * LANES), BF16),
            pltpu.VMEM((12 * 3 * WIN, 2 * LANES), F32),
            pltpu.VMEM((3, 3, PROWS, LANES), F32),
            pltpu.VMEM((2, 2, 4, 16, LANES), F32),
            pltpu.VMEM((2, 2, 4, 16, LANES), F32),
            pltpu.VMEM((4, 16, LANES), F32),
            pltpu.VMEM((tail_count, 2, 16, LANES), F32),
            pltpu.VMEM((16, LANES), F32),
            pltpu.VMEM((4, 16, LANES), F32),
            pltpu.VMEM((6, 8, LANES), F32),
            pltpu.VMEM((2, 8, LANES), F32),
            pltpu.SemaphoreType.DMA((2, 2)),
            pltpu.SemaphoreType.DMA((6,)),
            pltpu.SemaphoreType.DMA((10,)),
            pltpu.SemaphoreType.DMA((3 + tail_count,)),
            pltpu.SemaphoreType.DMA((tail_count,)),
        ],
        compiler_params=pltpu.CompilerParams(
            collective_id=0, has_side_effects=True, vmem_limit_bytes=32 * 1024 * 1024
        ),
    )(
        zonal_length,
        zonal_state.reshape(flat_shape),
        zonal_courant.reshape(LANES, CELLS),
        zonal_owner,
        merid_state.reshape(flat_shape),
        merid_courant.reshape(LANES, CELLS),
        mixing.reshape(LANES, 32),
    )
    return (
        out_z.reshape(zonal_state.shape),
        out_m.reshape(merid_state.shape),
        out_c.reshape(GLON_DEV, 4, LANES),
    )


def solution(mesh):
    counts = (mesh.shape["lon"], mesh.shape["lat"])
    return jax.shard_map(
        functools.partial(shards, counts),
        mesh=mesh,
        in_specs=(
            P(None, None, None, "lat", "lon"),
            P(None, "lat", "lon"),
            P("lat"),
            P("lat", "lon"),
            P(None, None, None, "lon", "lat"),
            P(None, "lon", "lat"),
            P(),
        ),
        out_specs=(
            P(None, None, None, "lat", "lon"),
            P(None, None, None, "lon", "lat"),
            P("lon", "lat", None),
        ),
        check_vma=False,
    )
```

profile of v0, /device:TPU:4, one launch (start us, length us, event | category | flops | bytes accessed | tf_op | source)
XLA Modules:
  0.0 29.7 jit_solution(9070045011232329678)
XLA Ops:
  0.6 0.0 copy-start.5
  0.6 0.0 copy-start.6
  0.7 0.7 %copy-done.5 = s32[4,128]{1,0:T(4,128)S(1)} copy-done((s32[4,128]{1,0:T(4,128)S(1)}, s32[4,128]{1,0:T(4,128)}, u32[]{:S(2)}) %copy-start.5) | copy-done | bytes 2072
  1.3 0.0 copy-done.6
  1.3 0.0 copy-start
  1.3 1.1 %copy-done = f32[4,32,3,4,128]{4,3,2,1,0:T(4,128)S(1)} copy-done((f32[4,32,3,4,128]{4,3,2,1,0:T(4,128)S(1)}, f32[4,32,3,4,128]{4,3,2,1,0:T(4,128)}, u32[]{:S(2)}) %copy-start) | copy-done | bytes 786456
  2.5 0.0 copy-start.1
  2.5 1.1 %copy-done.1 = f32[4,32,3,4,128]{4,3,2,1,0:T(4,128)S(1)} copy-done((f32[4,32,3,4,128]{4,3,2,1,0:T(4,128)S(1)}, f32[4,32,3,4,128]{4,3,2,1,0:T(4,128)}, u32[]{:S(2)}) %copy-start.1) | copy-done | bytes 786456
  3.6 0.0 copy-start.2
  3.6 0.8 %copy-done.2 = f32[32,4,128]{2,1,0:T(4,128)S(1)} copy-done((f32[32,4,128]{2,1,0:T(4,128)S(1)}, f32[32,4,128]{2,1,0:T(4,128)}, u32[]{:S(2)}) %copy-start.2) | copy-done | bytes 65560
  4.4 0.0 copy-start.3
  4.4 0.8 %copy-done.3 = f32[32,4,128]{2,1,0:T(4,128)S(1)} copy-done((f32[32,4,128]{2,1,0:T(4,128)S(1)}, f32[32,4,128]{2,1,0:T(4,128)}, u32[]{:S(2)}) %copy-start.3) | copy-done | bytes 65560
  5.3 0.0 copy-start.4
  5.3 0.8 %copy-done.4 = f32[4,32,32]{2,1,0:T(8,128)S(1)} copy-done((f32[4,32,32]{2,1,0:T(8,128)S(1)}, f32[4,32,32]{2,1,0:T(8,128)}, u32[]{:S(2)}) %copy-start.4) | copy-done | bytes 16408
  6.1 21.2 %shard_map.94 = (f32[1536,128]{1,0:T(8,128)S(1)}, f32[1536,128]{1,0:T(8,128)S(1)}, f32[16,128]{1,0:T(8,128)S(1)}) custom-call(s32[4]{0:T(128)S(1)} %copy-done.6, f32[1536,128]{1,0:T(8,128)S(1)} %bitcast.8, f32[128,128]{1,0:T(8,128)S(1)} %bitcast.12, s32[4,128]{1,0:T(4,128)S(1)} %copy-done.5, f32[1536,128]{1,0:T(8,128)S(1)} %bitcast.9, ...), custom_call_target="tpu_custom_call" | custom-call | tf_op jit(solution)/shard_map/pallas_call | solution.py:464
  27.3 0.9 %copy.13 = f32[4,32,3,4,128]{4,3,2,1,0:T(4,128)} copy(f32[4,32,3,4,128]{4,3,2,1,0:T(4,128)S(1)} %bitcast.11) | data formatting | bytes 1572864
  28.2 0.9 %copy.14 = f32[4,32,3,4,128]{4,3,2,1,0:T(4,128)} copy(f32[4,32,3,4,128]{4,3,2,1,0:T(4,128)S(1)} %bitcast.10) | data formatting | bytes 1572864
  29.1 0.6 %copy.15 = f32[4,4,128]{2,1,0:T(4,128)} copy(f32[4,4,128]{2,1,0:T(4,128)S(1)} %bitcast.15) | data formatting | bytes 16384
Async XLA Ops:
  0.6 0.7 %copy-start.5 = (s32[4,128]{1,0:T(4,128)S(1)}, s32[4,128]{1,0:T(4,128)}, u32[]{:S(2)}) copy-start(s32[4,128]{1,0:T(4,128)} %owner.1) | copy-start | bytes 6148
  0.6 0.7 %copy-start.6 = (s32[4]{0:T(128)S(1)}, s32[4]{0:T(128)}, u32[]{:S(2)}) copy-start(s32[4]{0:T(128)} %zlen.1) | copy-start | bytes 52
  1.3 1.1 %copy-start = (f32[4,32,3,4,128]{4,3,2,1,0:T(4,128)S(1)}, f32[4,32,3,4,128]{4,3,2,1,0:T(4,128)}, u32[]{:S(2)}) copy-start(f32[4,32,3,4,128]{4,3,2,1,0:T(4,128)} %param.7) | copy-start | bytes 2359300
  2.5 1.1 %copy-start.1 = (f32[4,32,3,4,128]{4,3,2,1,0:T(4,128)S(1)}, f32[4,32,3,4,128]{4,3,2,1,0:T(4,128)}, u32[]{:S(2)}) copy-start(f32[4,32,3,4,128]{4,3,2,1,0:T(4,128)} %param.11) | copy-start | bytes 2359300
  3.6 0.8 %copy-start.2 = (f32[32,4,128]{2,1,0:T(4,128)S(1)}, f32[32,4,128]{2,1,0:T(4,128)}, u32[]{:S(2)}) copy-start(f32[32,4,128]{2,1,0:T(4,128)} %param.8) | copy-start | bytes 196612
  4.4 0.8 %copy-start.3 = (f32[32,4,128]{2,1,0:T(4,128)S(1)}, f32[32,4,128]{2,1,0:T(4,128)}, u32[]{:S(2)}) copy-start(f32[32,4,128]{2,1,0:T(4,128)} %param.12) | copy-start | bytes 196612
  5.3 0.8 %copy-start.4 = (f32[4,32,32]{2,1,0:T(8,128)S(1)}, f32[4,32,32]{2,1,0:T(8,128)}, u32[]{:S(2)}) copy-start(f32[4,32,32]{2,1,0:T(8,128)} %param.13) | copy-start | bytes 49156
where the time goes:
time: 30 us; the launch traced here: 29.7 us
  Pallas kernels  21.2 us (71%)
  local copies, waits for them, and re-layouts  7.81 us (26%)
  between operations  0.66 us (2%)
    pallas_call x1, Pallas kernels, shards(): pl.pallas_call(functools.partial(kernel, counts), out_shape=(jax.ShapeDty...  21.2 us
    unnamed x17, local copies, waits for them, and re-layouts  7.81 us

commit v1 on v0

--- a/solution.py
+++ b/solution.py
@@ -59,18 +59,21 @@
 
 def kernel(
     counts,
-    zlen,
+    zlen_ref,
     zs,
     zc,
-    owner,
+    owner_ref,
     ms,
     mc,
-    mix,
+    mix_ref,
     out_z,
     out_m,
     out_c,
     raw,
     rawc,
+    owner,
+    mix,
+    zlen,
     first,
     state,
     weights,
@@ -129,9 +132,48 @@
     for f, (s_ref, c_ref) in enumerate(((zs, zc), (ms, mc))):
         loads.append(pltpu.make_async_copy(s_ref, raw.at[f], load_sem.at[f, 0]))
         loads.append(pltpu.make_async_copy(c_ref, rawc.at[f], load_sem.at[f, 1]))
+    loads.append(pltpu.make_async_copy(mix_ref, mix, load_sem.at[2, 0]))
+    loads.append(pltpu.make_async_copy(owner_ref, owner, load_sem.at[2, 1]))
+    loads.append(pltpu.make_async_copy(zlen_ref, zlen, load_sem.at[3, 0]))
     for load in loads:
         load.start()
 
+    def turn_in(f, channels):
+        if channels[0] != 1:
+            loads[2 * f].wait()
+            loads[2 * f + 1].wait()
+        for r in channels:
+            for w in range(3):
+                turned = raw[f, pl.ds(w * 4 + r, LANES, stride=12), :].T
+                first[4 * f + r, w, OFF : OFF + CELLS, :] = turned
+                state[0, 4 * f + r, w, OFF : OFF + CELLS, :] = turned
+            c_now = rawc[f, pl.ds(r, 32, stride=4), :]
+            first[4 * f + r, 3, OFF : OFF + CELLS, :] = jnp.concatenate([c_now] * 4, axis=0).T
+        for r in channels:
+            for p in range(4):
+                edges[f, 0, r, 4 * p : 4 * p + 4, :] = first[4 * f + r, p, OFF : OFF + SUB, :]
+                edges[f, 1, r, 4 * p : 4 * p + 4, :] = first[
+                    4 * f + r, p, OFF + CELLS - SUB : OFF + CELLS, :
+                ]
+
+    with jax.named_scope("turn_z"):
+        turn_in(0, (2, 3, 0))
+        loads[6].wait()
+        ends = [jnp.clip(zlen[r] - me * CELLS, 0, CELLS + SUB) for r in range(4)]
+        quarter = lax.broadcasted_iota(jnp.int32, (8, LANES), 0)
+        for r in FAR:
+            cell = ends[r] - SUB + quarter
+            own = (cell >= 0) & (cell < CELLS)
+            for p in range(4):
+                found = jnp.where(own, first[r, p, pl.ds(OFF + ends[r] - SUB, 8), :], 0.0)
+                tails[r, 4 * p : 4 * p + 4, :] = found[0:SUB]
+        turn_in(0, (1,))
+
+    with jax.named_scope("turn_m"):
+        turn_in(1, (0, 1, 2, 3))
+
+    loads[4].wait()
+    loads[5].wait()
     spread = jnp.concatenate([mix[...]] * 4, axis=1)
     row_at = lax.broadcasted_iota(jnp.int32, (LANES, LANES), 0)
     lane_at = lax.broadcasted_iota(jnp.int32, (LANES, LANES), 1)
@@ -142,36 +184,11 @@
         weights[row : row + LANES, 0:LANES] = high
         weights[row : row + LANES, LANES:] = low
 
-    def turn_in(f):
-        loads[2 * f].wait()
-        loads[2 * f + 1].wait()
-        for r in range(4):
-            for w in range(3):
-                turned = raw[f, pl.ds(w * 4 + r, LANES, stride=12), :].T
-                first[4 * f + r, w, OFF : OFF + CELLS, :] = turned
-                state[0, 4 * f + r, w, OFF : OFF + CELLS, :] = turned
-            c_now = rawc[f, pl.ds(r, 32, stride=4), :]
-            first[4 * f + r, 3, OFF : OFF + CELLS, :] = jnp.concatenate([c_now] * 4, axis=0).T
-        for r in range(4):
-            for p in range(4):
-                edges[f, 0, r, 4 * p : 4 * p + 4, :] = first[4 * f + r, p, OFF : OFF + SUB, :]
-                edges[f, 1, r, 4 * p : 4 * p + 4, :] = first[
-                    4 * f + r, p, OFF + CELLS - SUB : OFF + CELLS, :
-                ]
-
-    turn_in(0)
-    ends = [jnp.clip(zlen[r] - me * CELLS, 0, CELLS + SUB) for r in range(4)]
-    quarter = lax.broadcasted_iota(jnp.int32, (8, LANES), 0)
-    for r in FAR:
-        cell = ends[r] - SUB + quarter
-        own = (cell >= 0) & (cell < CELLS)
-        for p in range(4):
-            found = jnp.where(own, first[r, p, pl.ds(OFF + ends[r] - SUB, 8), :], 0.0)
-            tails[r, 4 * p : 4 * p + 4, :] = found[0:SUB]
-    turn_in(1)
-
-    def interior(f):
+
+    def interior(f, between=None):
         def step(t, carry):
+            if between is not None:
+                pl.when(is_root & (t == 2))(between)
             now, then = lax.rem(t, 2), lax.rem(t + 1, 2)
 
             def src(ch, w, at, size):
@@ -195,11 +212,6 @@
             return carry
 
         lax.fori_loop(0, SUB, step, 0)
-
-    interior(0)
-
-    peers = 4 + jnp.where(is_tail, 1, 0) + jnp.where(is_root, len(tail_devs), 0)
-    pl.semaphore_wait(barrier, peers)
 
     def remote(src, dst, s_sem, r_sem, peer):
         return pltpu.make_async_remote_copy(
@@ -236,20 +248,6 @@
         {"lon": 0 * me + half_turn, "lat": lat},
     )
 
-    @pl.when(is_tail)
-    def _():
-        tail_copy.start()
-
-    @pl.when(is_half)
-    def _():
-        tail_0_copy.start()
-
-    @pl.when(is_root)
-    def _():
-        head_0_copy.start()
-        for copy in head_copies:
-            copy.start()
-
     south_side, north_side = jnp.where(at_south, 0, 1), jnp.where(at_north, 1, 0)
     near = [
         remote(edges.at[0, 0], halos.at[0, 1], send_sem.at[0], recv_sem.at[1], west),
@@ -269,10 +267,35 @@
             north,
         ),
     ]
-    for copy in near:
-        copy.start()
-
-    interior(1)
+    @pl.when(jnp.logical_not(is_root))
+    def _():
+        with jax.named_scope("barrier"):
+            pl.semaphore_wait(barrier, 4 + jnp.where(is_tail, 1, 0))
+
+        @pl.when(is_tail)
+        def _():
+            tail_copy.start()
+
+        @pl.when(is_half)
+        def _():
+            tail_0_copy.start()
+
+        for copy in near:
+            copy.start()
+
+    def root_sends():
+        with jax.named_scope("barrier_root"):
+            pl.semaphore_wait(barrier, 4 + len(tail_devs))
+        for copy in near:
+            copy.start()
+        head_0_copy.start()
+        for copy in head_copies:
+            copy.start()
+
+    with jax.named_scope("interior_z"):
+        interior(0)
+    with jax.named_scope("interior_m"):
+        interior(1, root_sends)
 
     def arrived(f, side):
         pltpu.make_async_copy(
@@ -311,8 +334,9 @@
         scour[n, :, :] = first[ch, 3, pl.ds(start, WIN), :]
 
     left_row, right_row = OFF - SUB, OFF + CELLS
-    for f, side in ((0, 0), (0, 1), (1, 0), (1, 1)):
-        arrived(f, side)
+    with jax.named_scope("near_wait"):
+        for f, side in ((0, 0), (0, 1), (1, 0), (1, 1)):
+            arrived(f, side)
     for r in range(4):
         for p in range(4):
             first[r, p, right_row : right_row + SUB, :] = halos[0, 1, r, 4 * p : 4 * p + 4, :]
@@ -333,7 +357,8 @@
         fill(r, r, right_start)
         fill(4 + r, 4 + r, left_start)
         fill(8 + r, 4 + r, right_start)
-    strip_steps(12)
+    with jax.named_scope("near_strips"):
+        strip_steps(12)
     for r in range(4):
         for w in range(3):
             kept = strips[0, r, w, OFF + 8 : OFF + 12, :]
@@ -348,19 +373,47 @@
                 0, 4 + r, w, OFF : OFF + CELLS, :
             ].T
 
+    near_columns = me * GLON_DEV - 1 + lax.broadcasted_iota(jnp.int32, (8, CELLS), 0)
+    column = lax.broadcasted_iota(jnp.int32, (CELLS, LANES), 0)
+    scale = GLON_DEV / (3.0 * CELLS)
+    back_copy = remote(part.at[4], part_in.at[1], send_sem.at[4], recv_sem.at[5], west)
+    on_copy = remote(part.at[5], part_in.at[0], send_sem.at[5], recv_sem.at[4], east)
+    is_last = me == lon_count - 1
+
+    def shares(r, change):
+        high, low = two_parts(change * scale)
+        mine = (jnp.broadcast_to(owner[r : r + 1, :], (8, CELLS)) == near_columns).astype(BF16)
+        return jnp.dot(
+            jnp.concatenate([mine, mine], axis=1),
+            jnp.concatenate([high, low], axis=0),
+            preferred_element_type=F32,
+        )
+
     @pl.when(is_root)
     def _():
-        for n in range(len(tail_devs)):
-            pltpu.make_async_copy(gathered.at[n], gathered.at[n], far_recv.at[n]).wait()
-        pltpu.make_async_copy(gathered_0, gathered_0, recv_sem.at[7]).wait()
-
-    @pl.when(is_tail)
-    def _():
-        pltpu.make_async_copy(heads.at[2:4], heads.at[2:4], recv_sem.at[8]).wait()
-
-    @pl.when(is_half)
-    def _():
-        pltpu.make_async_copy(heads.at[0], heads.at[0], recv_sem.at[9]).wait()
+        with jax.named_scope("early_part"):
+            for r in range(4):
+                change = None
+                for w in range(3):
+                    value = state[0, r, w, OFF : OFF + CELLS, :] - first[r, w, OFF : OFF + CELLS, :]
+                    change = value if change is None else change + value
+                part[5, r : r + 1, :] = shares(r, change)[5:6]
+            on_copy.start()
+
+    with jax.named_scope("far_wait"):
+        @pl.when(is_root)
+        def _():
+            for n in range(len(tail_devs)):
+                pltpu.make_async_copy(gathered.at[n], gathered.at[n], far_recv.at[n]).wait()
+            pltpu.make_async_copy(gathered_0, gathered_0, recv_sem.at[7]).wait()
+
+        @pl.when(is_tail)
+        def _():
+            pltpu.make_async_copy(heads.at[2:4], heads.at[2:4], recv_sem.at[8]).wait()
+
+        @pl.when(is_half)
+        def _():
+            pltpu.make_async_copy(heads.at[0], heads.at[0], recv_sem.at[9]).wait()
 
     for r in range(4):
         if r == 1:
@@ -383,7 +436,8 @@
         for w in range(3):
             strips[0, 4 + n, w, OFF + 8 : OFF + 12, :] = heads[r, 4 * w : 4 * w + 4, :]
         scour[4 + n, 8:12, :] = heads[r, 12:16, :]
-    strip_steps(7)
+    with jax.named_scope("far_strips"):
+        strip_steps(7)
     for r in range(4):
         for w in range(3):
             kept = strips[0, r, w, OFF + 4 : OFF + 8, :]
@@ -392,9 +446,6 @@
         for w in range(3):
             back[n, w, PBASE : PBASE + WIN, :] = strips[0, 4 + n, w, OFF : OFF + WIN, :]
 
-    near_columns = me * GLON_DEV - 1 + lax.broadcasted_iota(jnp.int32, (8, CELLS), 0)
-    column = lax.broadcasted_iota(jnp.int32, (CELLS, LANES), 0)
-    scale = GLON_DEV / (3.0 * CELLS)
     for r in range(4):
         change = None
         for w in range(3):
@@ -408,22 +459,38 @@
                 value = jnp.where(column < cut, value, before)
             out_z[pl.ds(w * 4 + r, LANES, stride=12), :] = value.T
             change = value - before if change is None else change + (value - before)
-        high, low = two_parts(change * scale)
-        mine = (jnp.broadcast_to(owner[r : r + 1, :], (8, CELLS)) == near_columns).astype(BF16)
-        part[r, :, :] = jnp.dot(
-            jnp.concatenate([mine, mine], axis=1),
-            jnp.concatenate([high, low], axis=0),
-            preferred_element_type=F32,
-        )
-    for r in range(4):
-        part[4, r : r + 1, :] = part[r, 0:1, :]
-        part[5, r : r + 1, :] = part[r, 5:6, :]
-    back_copy = remote(part.at[4], part_in.at[1], send_sem.at[4], recv_sem.at[5], west)
-    on_copy = remote(part.at[5], part_in.at[0], send_sem.at[5], recv_sem.at[4], east)
-    back_copy.start()
-    on_copy.start()
-    back_copy.wait_recv()
-    on_copy.wait_recv()
+        part[r, :, :] = shares(r, change)
+
+    @pl.when(jnp.logical_not(is_root))
+    def _():
+        for r in range(4):
+            part[4, r : r + 1, :] = part[r, 0:1, :]
+        back_copy.start()
+
+    @pl.when(jnp.logical_not(is_root | is_last))
+    def _():
+        for r in range(4):
+            part[5, r : r + 1, :] = part[r, 5:6, :]
+        on_copy.start()
+
+    with jax.named_scope("part_wait"):
+
+        @pl.when(is_root)
+        def _():
+            part_in[0, :, :] = jnp.zeros((8, LANES), F32)
+
+        @pl.when(is_last)
+        def _():
+            part_in[1, :, :] = jnp.zeros((8, LANES), F32)
+
+        @pl.when(jnp.logical_not(is_last))
+        def _():
+            back_copy.wait_recv()
+
+        @pl.when(jnp.logical_not(is_root))
+        def _():
+            on_copy.wait_recv()
+
     for r in range(4):
         for g in range(GLON_DEV):
             value = part[r, g + 1 : g + 2, :]
@@ -435,8 +502,14 @@
 
     for copy in near:
         copy.wait_send()
-    back_copy.wait_send()
-    on_copy.wait_send()
+
+    @pl.when(jnp.logical_not(is_root))
+    def _():
+        back_copy.wait_send()
+
+    @pl.when(jnp.logical_not(is_last))
+    def _():
+        on_copy.wait_send()
 
     @pl.when(is_tail)
     def _():
@@ -451,6 +524,17 @@
         head_0_copy.wait_send()
         for copy in head_copies:
             copy.wait_send()
+
+
+def write_out(z, m, c, out_z, out_m, out_c, sem):
+    copies = [
+        pltpu.make_async_copy(src, dst, sem.at[n])
+        for n, (src, dst) in enumerate(((z, out_z), (m, out_m), (c, out_c)))
+    ]
+    for copy in copies:
+        copy.start()
+    for copy in copies:
+        copy.wait()
 
 
 def shards(
@@ -459,20 +543,26 @@
     tail_count = counts[0] - (counts[0] // 4 - 1)
     hbm = pl.BlockSpec(memory_space=pltpu.HBM)
     vmem = pl.BlockSpec(memory_space=pltpu.VMEM)
-    smem = pl.BlockSpec(memory_space=pltpu.SMEM)
     flat_shape = (LANES * 12, CELLS)
+
+    def in_hbm(array, shape):
+        return pltpu.with_memory_space_constraint(array.reshape(shape), pltpu.HBM)
+
     out_z, out_m, out_c = pl.pallas_call(
         functools.partial(kernel, counts),
         out_shape=(
-            jax.ShapeDtypeStruct(flat_shape, F32),
-            jax.ShapeDtypeStruct(flat_shape, F32),
-            jax.ShapeDtypeStruct((4 * GLON_DEV, LANES), F32),
+            pltpu.VMEM(flat_shape, F32),
+            pltpu.VMEM(flat_shape, F32),
+            pltpu.VMEM((4 * GLON_DEV, LANES), F32),
         ),
-        in_specs=[smem, hbm, hbm, vmem, hbm, hbm, vmem],
+        in_specs=[hbm, hbm, hbm, hbm, hbm, hbm, hbm],
         out_specs=(vmem, vmem, vmem),
         scratch_shapes=[
             pltpu.VMEM((2, *flat_shape), F32),
             pltpu.VMEM((2, LANES, CELLS), F32),
+            pltpu.VMEM((4, CELLS), jnp.int32),
+            pltpu.VMEM((LANES, 32), F32),
+            pltpu.SMEM((4,), jnp.int32),
             pltpu.VMEM((8, 4, ROWS, LANES), F32),
             pltpu.VMEM((2, 8, 3, ROWS, LANES), F32),
             pltpu.VMEM((2 * LANES, 2 * LANES), BF16),
@@ -491,7 +581,7 @@
             pltpu.VMEM((4, 16, LANES), F32),
             pltpu.VMEM((6, 8, LANES), F32),
             pltpu.VMEM((2, 8, LANES), F32),
-            pltpu.SemaphoreType.DMA((2, 2)),
+            pltpu.SemaphoreType.DMA((4, 2)),
             pltpu.SemaphoreType.DMA((6,)),
             pltpu.SemaphoreType.DMA((10,)),
             pltpu.SemaphoreType.DMA((3 + tail_count,)),
@@ -501,14 +591,26 @@
             collective_id=0, has_side_effects=True, vmem_limit_bytes=32 * 1024 * 1024
         ),
     )(
-        zonal_length,
-        zonal_state.reshape(flat_shape),
-        zonal_courant.reshape(LANES, CELLS),
-        zonal_owner,
-        merid_state.reshape(flat_shape),
-        merid_courant.reshape(LANES, CELLS),
-        mixing.reshape(LANES, 32),
+        in_hbm(zonal_length, (4,)),
+        in_hbm(zonal_state, flat_shape),
+        in_hbm(zonal_courant, (LANES, CELLS)),
+        in_hbm(zonal_owner, (4, CELLS)),
+        in_hbm(merid_state, flat_shape),
+        in_hbm(merid_courant, (LANES, CELLS)),
+        in_hbm(mixing, (LANES, 32)),
     )
+    out_z, out_m, out_c = pl.pallas_call(
+        write_out,
+        out_shape=(
+            pltpu.HBM(flat_shape, F32),
+            pltpu.HBM(flat_shape, F32),
+            pltpu.HBM((4 * GLON_DEV, LANES), F32),
+        ),
+        in_specs=[vmem, vmem, vmem],
+        out_specs=(hbm, hbm, hbm),
+        scratch_shapes=[pltpu.SemaphoreType.DMA((3,))],
+        compiler_params=pltpu.CompilerParams(vmem_limit_bytes=1024 * 1024),
+    )(out_z, out_m, out_c)
     return (
         out_z.reshape(zonal_state.shape),
         out_m.reshape(merid_state.shape),

time: 30 us -> 21.2 us (0.71)
  the two profiles are of different devices: /device:TPU:4 before, /device:TPU:6 now
where the time goes in v1:
time: 21.2 us; the launch traced here: 21.1 us
  Pallas kernels  20.5 us (97%)
  between operations  0.64 us (3%)
    pallas_call x1, Pallas kernels, shards(): pl.pallas_call(functools.partial(kernel, counts), out_shape=(pltpu.VMEM(f...  19.3 us
    pallas_call x1, Pallas kernels, shards(): pl.pallas_call(write_out, out_shape=(pltpu.HBM(flat_shape, F32), pltpu.HB...  1.17 us

profile of v1, /device:TPU:6, one launch (start us, length us, event | category | flops | bytes accessed | tf_op | source)
XLA Modules:
  0.0 21.1 jit_solution(14147913119190584890)
XLA Ops:
  0.6 19.3 %shard_map.94 = (f32[1536,128]{1,0:T(8,128)S(1)}, f32[1536,128]{1,0:T(8,128)S(1)}, f32[16,128]{1,0:T(8,128)S(1)}) custom-call(s32[4]{0:T(128)} %zlen_ref.1, f32[1536,128]{1,0:T(8,128)} %bitcast.8, f32[128,128]{1,0:T(8,128)} %bitcast.10, s32[4,128]{1,0:T(4,128)} %owner_ref.1, f32[1536,128]{1,0:T(8,128)} %bitcast.9, f32[128,128]{1,0:T(8,128)} %bitcast.11, ...), custom_call_target="tpu_custom_call" | custom-call | tf_op jit(solution)/shard_map/pallas_call | solution.py:551
  19.9 1.2 %shard_map.95 = (f32[1536,128]{1,0:T(8,128)}, f32[1536,128]{1,0:T(8,128)}, f32[16,128]{1,0:T(8,128)}) custom-call(f32[1536,128]{1,0:T(8,128)S(1)} %get-tuple-element.9.z, f32[1536,128]{1,0:T(8,128)S(1)} %get-tuple-element.10.m, f32[16,128]{1,0:T(8,128)S(1)} %get-tuple-element.11.c), custom_call_target="tpu_custom_call" | custom-call | tf_op jit(solution)/shard_map/pallas_call | solution.py:602

commit v2 on v1

v2 whole, which is shorter than its diff:
```python
import functools

import jax
import jax.numpy as jnp
from jax import lax
from jax.experimental import pallas as pl
from jax.experimental.pallas import tpu as pltpu
from jax.sharding import PartitionSpec as P

SUB = 4
OFF = 8
CELLS = 128
LANES = 128
ROWS = 152
WIN = 16
SROWS = 32
PROWS = 272
PBASE = 136
GLON_DEV = 4
FAR = (0, 2, 3)
MESH = pl.DeviceIdType.MESH
F32 = jnp.float32
BF16 = jnp.bfloat16


def two_parts(value):
    high = value.astype(BF16)
    low = (value - high.astype(F32)).astype(BF16)
    return high, low


def advance(src, dst, courant, weights, items, rows, chunk):
    group = max(1, CELLS // rows)
    for first_item in range(0, len(items), group):
        some = items[first_item : first_item + group]
        parts = [
            jnp.concatenate(two_parts(src(item, w, OFF, rows)), axis=1)
            for item in some
            for w in range(3)
        ]
        product = jnp.dot(
            jnp.concatenate(parts, axis=0), weights[...], preferred_element_type=F32
        )
        for n, item in enumerate(some):
            for at in range(0, rows, chunk):
                half = 0.5 * courant(item, at, chunk)
                ahead_share, behind_share = 0.3 - half, 0.3 + half
                here = [src(item, w, OFF + at, chunk) for w in range(3)]
                for w, (one, other) in enumerate(((0, 1), (0, 2), (1, 2))):
                    spot = (n * 3 + w) * rows + at
                    mixed = (
                        product[spot : spot + chunk, 0:LANES] + product[spot : spot + chunk, LANES:]
                    )
                    along = ahead_share * src(item, w, OFF + at + 1, chunk) + behind_share * src(
                        item, w, OFF + at - 1, chunk
                    )
                    dst(item, w, OFF + at, chunk, mixed + along + 0.1 * (here[one] + here[other]))


def relays_of(lon_count):
    tail_from, half_turn = lon_count // 4 - 1, lon_count // 2
    relays = {dev: [] for dev in (half_turn - 1, lon_count - 1, half_turn)}
    relays[tail_from], relays[half_turn + tail_from] = [], []
    for first, last in ((tail_from, half_turn - 1), (half_turn + tail_from, lon_count - 1)):
        for dev in range(first + 1, last):
            relays[first if dev <= first + 2 else last].append(dev)
    for dev in range(half_turn + 1, half_turn + tail_from):
        relays[dev] = []
    return relays


def kernel(
    counts,
    zlen_ref,
    zs,
    zc,
    owner_ref,
    ms,
    mc,
    mix_ref,
    out_z,
    out_m,
    out_c,
    raw,
    rawc,
    owner,
    mix,
    zlen,
    first,
    state,
    other_state,
    weights,
    strips,
    other_strips,
    scour,
    back,
    edges,
    halos,
    tails,
    gathered,
    gathered_0,
    heads,
    part,
    part_in,
    load_sem,
    send_sem,
    recv_sem,
    far_send,
    far_recv,
):
    lon_count, lat_count = counts
    half_turn = lon_count // 2
    tail_from = lon_count // 4 - 1
    tail_devs = list(range(tail_from, lon_count))
    relays = relays_of(lon_count)
    me, lat = lax.axis_index("lon"), lax.axis_index("lat")
    left = lax.rem(me + lon_count - 1, lon_count)
    right = lax.rem(me + 1, lon_count)
    across = lax.rem(me + half_turn, lon_count)
    at_south, at_north = lat == 0, lat == lat_count - 1
    south = {"lon": jnp.where(at_south, across, me), "lat": jnp.where(at_south, lat, lat - 1)}
    north = {"lon": jnp.where(at_north, across, me), "lat": jnp.where(at_north, lat, lat + 1)}
    west, east = {"lon": left, "lat": lat}, {"lon": right, "lat": lat}
    root = {"lon": 0 * me, "lat": lat}
    is_root, is_tail, is_half = me == 0, me >= tail_from, me == half_turn

    barrier = pltpu.get_barrier_semaphore()
    for peer in (west, east, south, north):
        pl.semaphore_signal(barrier, inc=1, device_id=peer, device_id_type=MESH)

    def sector(dev):
        return {"lon": 0 * me + dev, "lat": lat}

    child_count = 0 * me
    for relay, children in relays.items():
        child_count = child_count + jnp.where(me == relay, len(children), 0)

        @pl.when(me == relay)
        def _():
            pl.semaphore_signal(barrier, inc=1, device_id=root, device_id_type=MESH)

        if children:

            @pl.when((me >= children[0]) & (me <= children[-1]))
            def _(relay=relay):
                pl.semaphore_signal(
                    barrier, inc=1, device_id=sector(relay), device_id_type=MESH
                )

    peers = 4 + jnp.where(is_tail, 1, 0) + child_count + jnp.where(is_root, len(relays), 0)

    @pl.when(is_root)
    def _():
        for dev in tail_devs:
            pl.semaphore_signal(
                barrier, inc=1, device_id={"lon": 0 * me + dev, "lat": lat}, device_id_type=MESH
            )

    loads = []
    for f, (s_ref, c_ref) in enumerate(((zs, zc), (ms, mc))):
        loads.append(pltpu.make_async_copy(s_ref, raw.at[f], load_sem.at[f, 0]))
        loads.append(pltpu.make_async_copy(c_ref, rawc.at[f], load_sem.at[f, 1]))
    loads.append(pltpu.make_async_copy(mix_ref, mix, load_sem.at[2, 0]))
    loads.append(pltpu.make_async_copy(owner_ref, owner, load_sem.at[2, 1]))
    loads.append(pltpu.make_async_copy(zlen_ref, zlen, load_sem.at[3, 0]))
    for load in loads:
        load.start()

    def turn_in(f, channels):
        if channels[0] != 1:
            loads[2 * f].wait()
            loads[2 * f + 1].wait()
        for r in channels:
            for w in range(3):
                turned = raw[f, pl.ds(w * 4 + r, LANES, stride=12), :].T
                first[4 * f + r, w, OFF : OFF + CELLS, :] = turned
                state[4 * f + r, w, OFF : OFF + CELLS, :] = turned
            c_now = rawc[f, pl.ds(r, 32, stride=4), :]
            first[4 * f + r, 3, OFF : OFF + CELLS, :] = jnp.concatenate([c_now] * 4, axis=0).T
        for r in channels:
            for p in range(4):
                edges[f, 0, r, 4 * p : 4 * p + 4, :] = first[4 * f + r, p, OFF : OFF + SUB, :]
                edges[f, 1, r, 4 * p : 4 * p + 4, :] = first[
                    4 * f + r, p, OFF + CELLS - SUB : OFF + CELLS, :
                ]

    with jax.named_scope("turn_z"):
        turn_in(0, (2, 3, 0))
        loads[6].wait()
        ends = [jnp.clip(zlen[r] - me * CELLS, 0, CELLS + SUB) for r in range(4)]
        quarter = lax.broadcasted_iota(jnp.int32, (8, LANES), 0)
        for r in FAR:
            cell = ends[r] - SUB + quarter
            own = (cell >= 0) & (cell < CELLS)
            for p in range(4):
                found = jnp.where(own, first[r, p, pl.ds(OFF + ends[r] - SUB, 8), :], 0.0)
                tails[r, 4 * p : 4 * p + 4, :] = found[0:SUB]
        turn_in(0, (1,))

    def remote(src, dst, s_sem, r_sem, peer):
        return pltpu.make_async_remote_copy(
            src_ref=src,
            dst_ref=dst,
            send_sem=s_sem,
            recv_sem=r_sem,
            device_id=peer,
            device_id_type=MESH,
        )

    slot = jnp.maximum(me - tail_from, 0)
    tail_copy = remote(
        tails.at[2:4], gathered.at[slot], far_send.at[0], far_recv.at[slot], root
    )
    tail_0_copy = remote(
        tails.at[0], gathered_0, far_send.at[1], recv_sem.at[7], root
    )
    head_copies = [
        remote(
            edges.at[0, 0, 2:4], heads.at[2:4], far_send.at[2 + n], recv_sem.at[8], sector(relay)
        )
        for n, relay in enumerate(relays)
    ]
    head_0_copy = remote(
        edges.at[0, 0, 0], heads.at[0], far_send.at[1], recv_sem.at[9], sector(half_turn)
    )
    passed_on = {
        relay: [
            remote(heads.at[2:4], heads.at[2:4], far_send.at[2 + n], recv_sem.at[8], sector(dev))
            for n, dev in enumerate(children)
        ]
        for relay, children in relays.items()
    }

    south_side, north_side = jnp.where(at_south, 0, 1), jnp.where(at_north, 1, 0)
    near = [
        remote(edges.at[0, 0], halos.at[0, 1], send_sem.at[0], recv_sem.at[1], west),
        remote(edges.at[0, 1], halos.at[0, 0], send_sem.at[1], recv_sem.at[0], east),
        remote(
            edges.at[1, 0],
            halos.at[1, south_side],
            send_sem.at[2],
            recv_sem.at[2 + south_side],
            south,
        ),
        remote(
            edges.at[1, 1],
            halos.at[1, north_side],
            send_sem.at[3],
            recv_sem.at[2 + north_side],
            north,
        ),
    ]
    place = lax.rem(me, half_turn)
    is_late, is_early, is_mid = place >= half_turn // 2, place == 0, place == tail_from

    def entered():
        with jax.named_scope("barrier"):
            pl.semaphore_wait(barrier, peers)

        @pl.when(is_tail)
        def _():
            tail_copy.start()

        @pl.when(is_half)
        def _():
            tail_0_copy.start()

        for copy in near[:2]:
            copy.start()

    def then_send():
        for copy in near[2:]:
            copy.start()

        @pl.when(is_root)
        def _():
            for copy in head_copies:
                copy.start()
            head_0_copy.start()

    @pl.when(jnp.logical_not(is_early | is_mid))
    def _():
        entered()

    with jax.named_scope("turn_m"):
        turn_in(1, (0, 1, 2, 3))

    loads[4].wait()
    loads[5].wait()
    spread = jnp.concatenate([mix[...]] * 4, axis=1)
    row_at = lax.broadcasted_iota(jnp.int32, (LANES, LANES), 0)
    lane_at = lax.broadcasted_iota(jnp.int32, (LANES, LANES), 1)
    spread = jnp.where(row_at // 32 == lane_at // 32, spread, 0.0)
    spread = spread + jnp.where(row_at == lane_at, 0.2, 0.0)
    high, low = two_parts(spread.T)
    for row in (0, LANES):
        weights[row : row + LANES, 0:LANES] = high
        weights[row : row + LANES, LANES:] = low

    def one_way(there, back, courant, items, rows, chunk):
        def src(item, w, at, size):
            return there[item, w, pl.ds(at, size), :]

        def dst(item, w, at, size, value):
            back[item, w, pl.ds(at, size), :] = value

        advance(src, dst, courant, weights, items, rows, chunk)

    def two_steps(there, back, courant, items, rows, chunk):
        one_way(there, back, courant, items, rows, chunk)
        one_way(back, there, courant, items, rows, chunk)

    def interior(f):
        items = [4 * f + r for r in range(4)]

        def courant(ch, at, size):
            return first[ch, 3, pl.ds(OFF + at, size), :]

        def step(t, carry):
            two_steps(state, other_state, courant, items, CELLS, 16)
            return carry

        lax.fori_loop(0, SUB // 2, step, 0)

    def arrived(f, side):
        pltpu.make_async_copy(
            halos.at[f, side], halos.at[f, side], recv_sem.at[2 * f + side]
        ).wait()

    def strip_steps(count):
        def step(t, carry):
            two_steps(
                strips,
                other_strips,
                lambda n, at, size: scour[n, pl.ds(at, size), :],
                list(range(count)),
                WIN,
                16,
            )
            return carry

        lax.fori_loop(0, SUB // 2, step, 0)

    def fill(n, ch, start):
        for w in range(3):
            strips[n, w, OFF : OFF + WIN, :] = first[ch, w, pl.ds(start, WIN), :]
        scour[n, :, :] = first[ch, 3, pl.ds(start, WIN), :]

    left_row, right_row = OFF - SUB, OFF + CELLS
    left_start, right_start = OFF - SUB, OFF + CELLS + SUB - WIN
    near_columns = me * GLON_DEV - 1 + lax.broadcasted_iota(jnp.int32, (8, CELLS), 0)
    column = lax.broadcasted_iota(jnp.int32, (CELLS, LANES), 0)
    scale = GLON_DEV / (3.0 * CELLS)
    back_copy = remote(part.at[4], part_in.at[1], send_sem.at[4], recv_sem.at[5], west)
    on_copy = remote(part.at[5], part_in.at[0], send_sem.at[5], recv_sem.at[4], east)
    is_last = me == lon_count - 1

    def merid_end():
        with jax.named_scope("merid_wait"):
            arrived(1, 0)
            arrived(1, 1)
        for side, turned, row in ((0, at_south, left_row), (1, at_north, right_row)):
            for r in range(4):
                for p in range(4):
                    plain = halos[1, side, r, 4 * p : 4 * p + 4, :]
                    q = p if p == 3 else 2 - p
                    mirrored = jnp.concatenate(
                        [halos[1, side, r, 4 * q + 3 - j : 4 * q + 4 - j, :] for j in range(SUB)],
                        axis=0,
                    )
                    if p == 3:
                        mirrored = -mirrored
                    first[4 + r, p, row : row + SUB, :] = jnp.where(turned, mirrored, plain)
        for r in range(4):
            fill(r, 4 + r, left_start)
            fill(4 + r, 4 + r, right_start)
        with jax.named_scope("merid_strips"):
            strip_steps(8)
        for r in range(4):
            for w in range(3):
                kept = strips[r, w, OFF + 4 : OFF + 8, :]
                state[4 + r, w, OFF : OFF + SUB, :] = kept
                kept = strips[4 + r, w, OFF + 8 : OFF + 12, :]
                state[4 + r, w, OFF + CELLS - SUB : OFF + CELLS, :] = kept
        for r in range(4):
            for w in range(3):
                out_m[pl.ds(w * 4 + r, LANES, stride=12), :] = state[
                    4 + r, w, OFF : OFF + CELLS, :
                ].T

    def shares(r, change):
        high, low = two_parts(change * scale)
        mine = (jnp.broadcast_to(owner[r : r + 1, :], (8, CELLS)) == near_columns).astype(BF16)
        return jnp.dot(
            jnp.concatenate([mine, mine], axis=1),
            jnp.concatenate([high, low], axis=0),
            preferred_element_type=F32,
        )

    def right_strips(at):
        for r in range(4):
            for p in range(4):
                first[r, p, right_row : right_row + SUB, :] = halos[0, 1, r, 4 * p : 4 * p + 4, :]
        for r in range(4):
            fill(at + r, r, right_start)

    def right_kept(at):
        for r in range(4):
            for w in range(3):
                kept = strips[at + r, w, OFF + 8 : OFF + 12, :]
                state[r, w, OFF + CELLS - SUB : OFF + CELLS, :] = kept

    is_relay = functools.reduce(jnp.logical_or, [me == relay for relay in relays])

    def heads_arrived():
        pltpu.make_async_copy(heads.at[2:4], heads.at[2:4], recv_sem.at[8]).wait()

    def pass_on():
        with jax.named_scope("pass_on"):
            for relay, copies in passed_on.items():

                @pl.when(me == relay)
                def _(copies=copies):
                    heads_arrived()
                    for copy in copies:
                        copy.start()

    def early_part():
        arrived(0, 1)
        with jax.named_scope("early_part"):
            right_strips(0)
            strip_steps(4)
            right_kept(0)
            for r in range(4):
                change = None
                for w in range(3):
                    value = (
                        state[r, w, OFF : OFF + CELLS, :] - first[r, w, OFF : OFF + CELLS, :]
                    )
                    change = value if change is None else change + value
                change = jnp.where(column >= SUB, change, 0.0)
                part[5, r : r + 1, :] = shares(r, change)[5:6]
            on_copy.start()

    def zonal_end(first_wait=True):
        if first_wait:
            with jax.named_scope("right_wait"):
                arrived(0, 1)

        with jax.named_scope("far_wait"):

            arrived(0, 0)

            @pl.when(is_tail & jnp.logical_not(is_relay))
            def _():
                heads_arrived()

            @pl.when(is_half)
            def _():
                pltpu.make_async_copy(heads.at[0], heads.at[0], recv_sem.at[9]).wait()

            @pl.when(is_root)
            def _():
                for n in range(len(tail_devs)):
                    pltpu.make_async_copy(gathered.at[n], gathered.at[n], far_recv.at[n]).wait()
                pltpu.make_async_copy(gathered_0, gathered_0, recv_sem.at[7]).wait()

        for r in range(4):
            for p in range(4):
                first[r, p, left_row : left_row + SUB, :] = halos[0, 0, r, 4 * p : 4 * p + 4, :]

        @pl.when(is_root)
        def _():
            for r in FAR:
                if r == 0:
                    tail_cells = gathered_0[...]
                else:
                    tail_cells = gathered[0, r - 2]
                    for n in range(1, len(tail_devs)):
                        tail_cells = tail_cells + gathered[n, r - 2]
                for p in range(4):
                    first[r, p, left_row : left_row + SUB, :] = tail_cells[4 * p : 4 * p + 4]

        right_strips(0)
        for r in range(4):
            fill(4 + r, r, left_start)
        for n, r in enumerate(FAR):
            fill(8 + n, r, ends[r])
            for w in range(3):
                strips[8 + n, w, OFF + 8 : OFF + 12, :] = heads[r, 4 * w : 4 * w + 4, :]
            scour[8 + n, 8:12, :] = heads[r, 12:16, :]
        with jax.named_scope("zonal_strips"):
            strip_steps(11)
        right_kept(0)
        for r in range(4):
            for w in range(3):
                kept = strips[4 + r, w, OFF + 4 : OFF + 8, :]
                state[r, w, OFF : OFF + SUB, :] = kept
        for n, r in enumerate(FAR):
            for w in range(3):
                back[n, w, PBASE : PBASE + WIN, :] = strips[8 + n, w, OFF : OFF + WIN, :]

        for r in range(4):
            change = None
            for w in range(3):
                value = state[r, w, OFF : OFF + CELLS, :]
                before = first[r, w, OFF : OFF + CELLS, :]
                if r in FAR:
                    n = FAR.index(r)
                    cut = ends[r]
                    strip = back[n, w, pl.ds(PBASE + 8 - cut, CELLS), :]
                    value = jnp.where(column >= cut - SUB, strip, value)
                    value = jnp.where(column < cut, value, before)
                    state[r, w, OFF : OFF + CELLS, :] = value
                change = value - before if change is None else change + (value - before)
            part[r, :, :] = shares(r, change)

        @pl.when(jnp.logical_not(is_root))
        def _():
            for r in range(4):
                part[4, r : r + 1, :] = part[r, 0:1, :]
            back_copy.start()

        @pl.when(jnp.logical_not(is_root | is_last))
        def _():
            for r in range(4):
                part[5, r : r + 1, :] = part[r, 5:6, :]
            on_copy.start()

    @pl.when(jnp.logical_not(is_early | is_mid))
    def _():
        then_send()

    @pl.when(is_late)
    def _():
        with jax.named_scope("interior_z"):
            interior(0)
        pass_on()
        zonal_end()
        with jax.named_scope("interior_m"):
            interior(1)
        merid_end()

    @pl.when(jnp.logical_not(is_late))
    def _():
        with jax.named_scope("interior_m"):
            interior(1)

        @pl.when(is_mid)
        def _():
            entered()
            then_send()

        with jax.named_scope("interior_z"):
            interior(0)

        @pl.when(is_early)
        def _():
            entered()
            then_send()

        @pl.when(is_root)
        def _():
            early_part()

        @pl.when(jnp.logical_not(is_root))
        def _():
            with jax.named_scope("right_wait"):
                arrived(0, 1)

        @pl.when(jnp.logical_not(is_early | is_mid) | is_root)
        def _():
            merid_end()

        pass_on()
        zonal_end(False)

        @pl.when((is_early | is_mid) & jnp.logical_not(is_root))
        def _():
            merid_end()

    for r in range(4):
        for w in range(3):
            out_z[pl.ds(w * 4 + r, LANES, stride=12), :] = state[r, w, OFF : OFF + CELLS, :].T

    with jax.named_scope("part_wait"):

        @pl.when(is_root)
        def _():
            part_in[0, :, :] = jnp.zeros((8, LANES), F32)

        @pl.when(is_last)
        def _():
            part_in[1, :, :] = jnp.zeros((8, LANES), F32)

        @pl.when(jnp.logical_not(is_last))
        def _():
            back_copy.wait_recv()

        @pl.when(jnp.logical_not(is_root))
        def _():
            on_copy.wait_recv()

    for r in range(4):
        for g in range(GLON_DEV):
            value = part[r, g + 1 : g + 2, :]
            if g == 0:
                value = value + part_in[0, r : r + 1, :]
            if g == GLON_DEV - 1:
                value = value + part_in[1, r : r + 1, :]
            out_c[4 * g + r : 4 * g + r + 1, :] = value

    for copy in near:
        copy.wait_send()

    @pl.when(jnp.logical_not(is_root))
    def _():
        back_copy.wait_send()

    @pl.when(jnp.logical_not(is_last))
    def _():
        on_copy.wait_send()

    @pl.when(is_tail)
    def _():
        tail_copy.wait_send()

    @pl.when(is_half)
    def _():
        tail_0_copy.wait_send()

    for relay, copies in passed_on.items():

        @pl.when(me == relay)
        def _(copies=copies):
            for copy in copies:
                copy.wait_send()

    @pl.when(is_root)
    def _():
        head_0_copy.wait_send()
        for copy in head_copies:
            copy.wait_send()


def write_out(z, m, c, out_z, out_m, out_c, sem):
    copies = [
        pltpu.make_async_copy(src, dst, sem.at[n])
        for n, (src, dst) in enumerate(((z, out_z), (m, out_m), (c, out_c)))
    ]
    for copy in copies:
        copy.start()
    for copy in copies:
        copy.wait()


def shards(
    counts, zonal_state, zonal_courant, zonal_length, zonal_owner, merid_state, merid_courant, mixing
):
    tail_count = counts[0] - (counts[0] // 4 - 1)
    relays = relays_of(counts[0])
    hbm = pl.BlockSpec(memory_space=pltpu.HBM)
    vmem = pl.BlockSpec(memory_space=pltpu.VMEM)
    flat_shape = (LANES * 12, CELLS)

    def in_hbm(array, shape):
        return pltpu.with_memory_space_constraint(array.reshape(shape), pltpu.HBM)

    out_z, out_m, out_c = pl.pallas_call(
        functools.partial(kernel, counts),
        out_shape=(
            pltpu.VMEM(flat_shape, F32),
            pltpu.VMEM(flat_shape, F32),
            pltpu.VMEM((4 * GLON_DEV, LANES), F32),
        ),
        in_specs=[hbm, hbm, hbm, hbm, hbm, hbm, hbm],
        out_specs=(vmem, vmem, vmem),
        scratch_shapes=[
            pltpu.VMEM((2, *flat_shape), F32),
            pltpu.VMEM((2, LANES, CELLS), F32),
            pltpu.VMEM((4, CELLS), jnp.int32),
            pltpu.VMEM((LANES, 32), F32),
            pltpu.SMEM((4,), jnp.int32),
            pltpu.VMEM((8, 4, ROWS, LANES), F32),
            pltpu.VMEM((8, 3, ROWS, LANES), F32),
            pltpu.VMEM((8, 3, ROWS, LANES), F32),
            pltpu.VMEM((2 * LANES, 2 * LANES), BF16),
            pltpu.VMEM((12, 3, SROWS, LANES), F32),
            pltpu.VMEM((12, 3, SROWS, LANES), F32),
            pltpu.VMEM((12, WIN, LANES), F32),
            pltpu.VMEM((3, 3, PROWS, LANES), F32),
            pltpu.VMEM((2, 2, 4, 16, LANES), F32),
            pltpu.VMEM((2, 2, 4, 16, LANES), F32),
            pltpu.VMEM((4, 16, LANES), F32),
            pltpu.VMEM((tail_count, 2, 16, LANES), F32),
            pltpu.VMEM((16, LANES), F32),
            pltpu.VMEM((4, 16, LANES), F32),
            pltpu.VMEM((6, 8, LANES), F32),
            pltpu.VMEM((2, 8, LANES), F32),
            pltpu.SemaphoreType.DMA((4, 2)),
            pltpu.SemaphoreType.DMA((6,)),
            pltpu.SemaphoreType.DMA((10,)),
            pltpu.SemaphoreType.DMA((2 + max(map(len, (relays, *relays.values()))),)),
            pltpu.SemaphoreType.DMA((tail_count,)),
        ],
        compiler_params=pltpu.CompilerParams(
            collective_id=0, has_side_effects=True, vmem_limit_bytes=32 * 1024 * 1024
        ),
    )(
        in_hbm(zonal_length, (4,)),
        in_hbm(zonal_state, flat_shape),
        in_hbm(zonal_courant, (LANES, CELLS)),
        in_hbm(zonal_owner, (4, CELLS)),
        in_hbm(merid_state, flat_shape),
        in_hbm(merid_courant, (LANES, CELLS)),
        in_hbm(mixing, (LANES, 32)),
    )
    out_z, out_m, out_c = pl.pallas_call(
        write_out,
        out_shape=(
            pltpu.HBM(flat_shape, F32),
            pltpu.HBM(flat_shape, F32),
            pltpu.HBM((4 * GLON_DEV, LANES), F32),
        ),
        in_specs=[vmem, vmem, vmem],
        out_specs=(hbm, hbm, hbm),
        scratch_shapes=[pltpu.SemaphoreType.DMA((3,))],
        compiler_params=pltpu.CompilerParams(vmem_limit_bytes=1024 * 1024),
    )(out_z, out_m, out_c)
    return (
        out_z.reshape(zonal_state.shape),
        out_m.reshape(merid_state.shape),
        out_c.reshape(GLON_DEV, 4, LANES),
    )


def solution(mesh):
    counts = (mesh.shape["lon"], mesh.shape["lat"])
    return jax.shard_map(
        functools.partial(shards, counts),
        mesh=mesh,
        in_specs=(
            P(None, None, None, "lat", "lon"),
            P(None, "lat", "lon"),
            P("lat"),
            P("lat", "lon"),
            P(None, None, None, "lon", "lat"),
            P(None, "lon", "lat"),
            P(),
        ),
        out_specs=(
            P(None, None, None, "lat", "lon"),
            P(None, None, None, "lon", "lat"),
            P("lon", "lat", None),
        ),
        check_vma=False,
    )
```

time: 21.2 us -> 18.4 us (0.87)
  the two profiles are of different devices: /device:TPU:6 before, /device:TPU:103 now
where the time goes in v2:
time: 18.4 us; the launch traced here: 18.3 us
  Pallas kernels  17.7 us (96%)
  between operations  0.64 us (3%)
    pallas_call x1, Pallas kernels, shards(): pl.pallas_call(functools.partial(kernel, counts), out_shape=(pltpu.VMEM(f...  16.5 us
    pallas_call x1, Pallas kernels, shards(): pl.pallas_call(write_out, out_shape=(pltpu.HBM(flat_shape, F32), pltpu.HB...  1.17 us

profile of v2, /device:TPU:103, one launch (start us, length us, event | category | flops | bytes accessed | tf_op | source)
XLA Modules:
  0.0 18.3 jit_solution(1569125699961904883)
XLA Ops:
  0.6 16.5 %shard_map.94 = (f32[1536,128]{1,0:T(8,128)S(1)}, f32[1536,128]{1,0:T(8,128)S(1)}, f32[16,128]{1,0:T(8,128)S(1)}) custom-call(s32[4]{0:T(128)} %zlen_ref.1, f32[1536,128]{1,0:T(8,128)} %bitcast.8, f32[128,128]{1,0:T(8,128)} %bitcast.10, s32[4,128]{1,0:T(4,128)} %owner_ref.1, f32[1536,128]{1,0:T(8,128)} %bitcast.9, f32[128,128]{1,0:T(8,128)} %bitcast.11, ...), custom_call_target="tpu_custom_call" | custom-call | tf_op jit(solution)/shard_map/pallas_call | solution.py:669
  17.1 1.2 %shard_map.95 = (f32[1536,128]{1,0:T(8,128)}, f32[1536,128]{1,0:T(8,128)}, f32[16,128]{1,0:T(8,128)}) custom-call(f32[1536,128]{1,0:T(8,128)S(1)} %get-tuple-element.9.z, f32[1536,128]{1,0:T(8,128)S(1)} %get-tuple-element.10.m, f32[16,128]{1,0:T(8,128)S(1)} %get-tuple-element.11.c), custom_call_target="tpu_custom_call" | custom-call | tf_op jit(solution)/shard_map/pallas_call | solution.py:718

commit v3 on v2

--- a/solution.py
+++ b/solution.py
@@ -107,6 +107,7 @@
     recv_sem,
     far_send,
     far_recv,
+    entry_sem,
 ):
     lon_count, lat_count = counts
     half_turn = lon_count // 2
@@ -124,38 +125,6 @@
     root = {"lon": 0 * me, "lat": lat}
     is_root, is_tail, is_half = me == 0, me >= tail_from, me == half_turn
 
-    barrier = pltpu.get_barrier_semaphore()
-    for peer in (west, east, south, north):
-        pl.semaphore_signal(barrier, inc=1, device_id=peer, device_id_type=MESH)
-
-    def sector(dev):
-        return {"lon": 0 * me + dev, "lat": lat}
-
-    child_count = 0 * me
-    for relay, children in relays.items():
-        child_count = child_count + jnp.where(me == relay, len(children), 0)
-
-        @pl.when(me == relay)
-        def _():
-            pl.semaphore_signal(barrier, inc=1, device_id=root, device_id_type=MESH)
-
-        if children:
-
-            @pl.when((me >= children[0]) & (me <= children[-1]))
-            def _(relay=relay):
-                pl.semaphore_signal(
-                    barrier, inc=1, device_id=sector(relay), device_id_type=MESH
-                )
-
-    peers = 4 + jnp.where(is_tail, 1, 0) + child_count + jnp.where(is_root, len(relays), 0)
-
-    @pl.when(is_root)
-    def _():
-        for dev in tail_devs:
-            pl.semaphore_signal(
-                barrier, inc=1, device_id={"lon": 0 * me + dev, "lat": lat}, device_id_type=MESH
-            )
-
     loads = []
     for f, (s_ref, c_ref) in enumerate(((zs, zc), (ms, mc))):
         loads.append(pltpu.make_async_copy(s_ref, raw.at[f], load_sem.at[f, 0]))
@@ -165,6 +134,48 @@
     loads.append(pltpu.make_async_copy(zlen_ref, zlen, load_sem.at[3, 0]))
     for load in loads:
         load.start()
+
+    place = lax.rem(me, half_turn)
+    is_late, is_early, is_mid = place >= half_turn // 2, place == 0, place == tail_from
+    answers = is_late & (lat == lat_count // 2 - 1)
+    asks = is_late & (lat == lat_count // 2)
+
+    barrier = pltpu.get_barrier_semaphore()
+    for peer in (west, east, south):
+        pl.semaphore_signal(barrier, inc=1, device_id=peer, device_id_type=MESH)
+
+    @pl.when(jnp.logical_not(answers))
+    def _():
+        pl.semaphore_signal(barrier, inc=1, device_id=north, device_id_type=MESH)
+
+    def sector(dev):
+        return {"lon": 0 * me + dev, "lat": lat}
+
+    child_count = 0 * me
+    for relay, children in relays.items():
+        child_count = child_count + jnp.where(me == relay, len(children), 0)
+
+        @pl.when(me == relay)
+        def _():
+            pl.semaphore_signal(barrier, inc=1, device_id=root, device_id_type=MESH)
+
+        if children:
+
+            @pl.when((me >= children[0]) & (me <= children[-1]))
+            def _(relay=relay):
+                pl.semaphore_signal(
+                    barrier, inc=1, device_id=sector(relay), device_id_type=MESH
+                )
+
+    zonal_first = (is_early | is_mid | (me < tail_from)) & (me != 0)
+    peers = 4 - jnp.where(asks, 1, 0) + jnp.where(is_tail, 1, 0) + child_count + jnp.where(is_root, len(relays), 0)
+
+    @pl.when(is_root)
+    def _():
+        for dev in tail_devs:
+            pl.semaphore_signal(
+                barrier, inc=1, device_id={"lon": 0 * me + dev, "lat": lat}, device_id_type=MESH
+            )
 
     def turn_in(f, channels):
         if channels[0] != 1:
@@ -250,13 +261,17 @@
             north,
         ),
     ]
-    place = lax.rem(me, half_turn)
-    is_late, is_early, is_mid = place >= half_turn // 2, place == 0, place == tail_from
-
-    def entered():
+    def entered(first_send=None):
         with jax.named_scope("barrier"):
             pl.semaphore_wait(barrier, peers)
 
+        if first_send is not None:
+            first_send()
+
+        @pl.when(answers)
+        def _():
+            pl.semaphore_signal(entry_sem, inc=1, device_id=north, device_id_type=MESH)
+
         @pl.when(is_tail)
         def _():
             tail_copy.start()
@@ -266,10 +281,6 @@
             tail_0_copy.start()
 
         for copy in near[:2]:
-            copy.start()
-
-    def then_send():
-        for copy in near[2:]:
             copy.start()
 
         @pl.when(is_root)
@@ -277,6 +288,13 @@
             for copy in head_copies:
                 copy.start()
             head_0_copy.start()
+
+    def then_send():
+        near[3].start()
+
+        @pl.when(jnp.logical_not(asks))
+        def _():
+            near[2].start()
 
     @pl.when(jnp.logical_not(is_early | is_mid))
     def _():
@@ -425,6 +443,12 @@
                     for copy in copies:
                         copy.start()
 
+    def left_kept(at):
+        for r in range(4):
+            for w in range(3):
+                kept = strips[at + r, w, OFF + 4 : OFF + 8, :]
+                state[r, w, OFF : OFF + SUB, :] = kept
+
     def early_part():
         arrived(0, 1)
         with jax.named_scope("early_part"):
@@ -447,30 +471,45 @@
             with jax.named_scope("right_wait"):
                 arrived(0, 1)
 
-        with jax.named_scope("far_wait"):
-
+        with jax.named_scope("left_wait"):
             arrived(0, 0)
-
-            @pl.when(is_tail & jnp.logical_not(is_relay))
-            def _():
-                heads_arrived()
-
-            @pl.when(is_half)
-            def _():
-                pltpu.make_async_copy(heads.at[0], heads.at[0], recv_sem.at[9]).wait()
-
-            @pl.when(is_root)
-            def _():
+        for r in range(4):
+            for p in range(4):
+                first[r, p, left_row : left_row + SUB, :] = halos[0, 0, r, 4 * p : 4 * p + 4, :]
+        right_strips(0)
+        for r in range(4):
+            fill(4 + r, r, left_start)
+        with jax.named_scope("zonal_strips"):
+            strip_steps(8)
+        right_kept(0)
+        left_kept(4)
+
+        @pl.when(is_tail)
+        def _():
+            with jax.named_scope("far_wait"):
+
+                @pl.when(jnp.logical_not(is_relay))
+                def _():
+                    heads_arrived()
+
+                @pl.when(is_half)
+                def _():
+                    pltpu.make_async_copy(heads.at[0], heads.at[0], recv_sem.at[9]).wait()
+
+            for n, r in enumerate(FAR):
+                fill(n, r, ends[r])
+                for w in range(3):
+                    strips[n, w, OFF + 8 : OFF + 12, :] = heads[r, 4 * w : 4 * w + 4, :]
+                scour[n, 8:12, :] = heads[r, 12:16, :]
+            with jax.named_scope("far_strips"):
+                strip_steps(3)
+
+        @pl.when(is_root)
+        def _():
+            with jax.named_scope("far_wait"):
                 for n in range(len(tail_devs)):
                     pltpu.make_async_copy(gathered.at[n], gathered.at[n], far_recv.at[n]).wait()
                 pltpu.make_async_copy(gathered_0, gathered_0, recv_sem.at[7]).wait()
-
-        for r in range(4):
-            for p in range(4):
-                first[r, p, left_row : left_row + SUB, :] = halos[0, 0, r, 4 * p : 4 * p + 4, :]
-
-        @pl.when(is_root)
-        def _():
             for r in FAR:
                 if r == 0:
                     tail_cells = gathered_0[...]
@@ -480,25 +519,15 @@
                         tail_cells = tail_cells + gathered[n, r - 2]
                 for p in range(4):
                     first[r, p, left_row : left_row + SUB, :] = tail_cells[4 * p : 4 * p + 4]
-
-        right_strips(0)
-        for r in range(4):
-            fill(4 + r, r, left_start)
-        for n, r in enumerate(FAR):
-            fill(8 + n, r, ends[r])
-            for w in range(3):
-                strips[8 + n, w, OFF + 8 : OFF + 12, :] = heads[r, 4 * w : 4 * w + 4, :]
-            scour[8 + n, 8:12, :] = heads[r, 12:16, :]
-        with jax.named_scope("zonal_strips"):
-            strip_steps(11)
-        right_kept(0)
-        for r in range(4):
-            for w in range(3):
-                kept = strips[4 + r, w, OFF + 4 : OFF + 8, :]
-                state[r, w, OFF : OFF + SUB, :] = kept
+            for r in range(4):
+                fill(r, r, left_start)
+            with jax.named_scope("far_strips"):
+                strip_steps(4)
+            left_kept(0)
+
         for n, r in enumerate(FAR):
             for w in range(3):
-                back[n, w, PBASE : PBASE + WIN, :] = strips[8 + n, w, OFF : OFF + WIN, :]
+                back[n, w, PBASE : PBASE + WIN, :] = strips[n, w, OFF : OFF + WIN, :]
 
         for r in range(4):
             change = None
@@ -536,6 +565,13 @@
         with jax.named_scope("interior_z"):
             interior(0)
         pass_on()
+
+        @pl.when(asks)
+        def _():
+            with jax.named_scope("answer_wait"):
+                pl.semaphore_wait(entry_sem, 1)
+            near[2].start()
+
         zonal_end()
         with jax.named_scope("interior_m"):
             interior(1)
@@ -546,36 +582,37 @@
         with jax.named_scope("interior_m"):
             interior(1)
 
-        @pl.when(is_mid)
-        def _():
-            entered()
-            then_send()
+        @pl.when(is_mid | is_early)
+        def _():
+            entered(then_send)
 
         with jax.named_scope("interior_z"):
             interior(0)
 
-        @pl.when(is_early)
-        def _():
-            entered()
-            then_send()
-
         @pl.when(is_root)
         def _():
             early_part()
+
+        @pl.when(is_early | is_mid)
+        def _():
+            pass_on()
 
         @pl.when(jnp.logical_not(is_root))
         def _():
             with jax.named_scope("right_wait"):
                 arrived(0, 1)
 
-        @pl.when(jnp.logical_not(is_early | is_mid) | is_root)
+        @pl.when(jnp.logical_not(zonal_first))
         def _():
             merid_end()
 
-        pass_on()
+        @pl.when(jnp.logical_not(is_early | is_mid))
+        def _():
+            pass_on()
+
         zonal_end(False)
 
-        @pl.when((is_early | is_mid) & jnp.logical_not(is_root))
+        @pl.when(zonal_first)
         def _():
             merid_end()
 
@@ -702,6 +739,7 @@
             pltpu.SemaphoreType.DMA((10,)),
             pltpu.SemaphoreType.DMA((2 + max(map(len, (relays, *relays.values()))),)),
             pltpu.SemaphoreType.DMA((tail_count,)),
+            pltpu.SemaphoreType.REGULAR,
         ],
         compiler_params=pltpu.CompilerParams(
             collective_id=0, has_side_effects=True, vmem_limit_bytes=32 * 1024 * 1024

time: 18.4 us -> 17.2 us (0.935)
  the two profiles are of different devices: /device:TPU:103 before, /device:TPU:59 now
where the time goes in v3:
time: 17.2 us; the launch traced here: 17.1 us
  Pallas kernels  16.5 us (96%)
  between operations  0.64 us (4%)
    pallas_call x1, Pallas kernels, shards(): pl.pallas_call(functools.partial(kernel, counts), out_shape=(pltpu.VMEM(f...  15.3 us
    pallas_call x1, Pallas kernels, shards(): pl.pallas_call(write_out, out_shape=(pltpu.HBM(flat_shape, F32), pltpu.HB...  1.17 us

profile of v3, /device:TPU:59, one launch (start us, length us, event | category | flops | bytes accessed | tf_op | source)
XLA Modules:
  0.0 17.1 jit_solution(14919209630521531293)
XLA Ops:
  0.6 15.3 %shard_map.94 = (f32[1536,128]{1,0:T(8,128)S(1)}, f32[1536,128]{1,0:T(8,128)S(1)}, f32[16,128]{1,0:T(8,128)S(1)}) custom-call(s32[4]{0:T(128)} %zlen_ref.1, f32[1536,128]{1,0:T(8,128)} %bitcast.8, f32[128,128]{1,0:T(8,128)} %bitcast.10, s32[4,128]{1,0:T(4,128)} %owner_ref.1, f32[1536,128]{1,0:T(8,128)} %bitcast.9, f32[128,128]{1,0:T(8,128)} %bitcast.11, ...), custom_call_target="tpu_custom_call" | custom-call | tf_op jit(solution)/shard_map/pallas_call | solution.py:706
  16.0 1.2 %shard_map.95 = (f32[1536,128]{1,0:T(8,128)}, f32[1536,128]{1,0:T(8,128)}, f32[16,128]{1,0:T(8,128)}) custom-call(f32[1536,128]{1,0:T(8,128)S(1)} %get-tuple-element.9.z, f32[1536,128]{1,0:T(8,128)S(1)} %get-tuple-element.10.m, f32[16,128]{1,0:T(8,128)S(1)} %get-tuple-element.11.c), custom_call_target="tpu_custom_call" | custom-call | tf_op jit(solution)/shard_map/pallas_call | solution.py:756

commit v4 on v3

--- a/solution.py
+++ b/solution.py
@@ -59,8 +59,8 @@
 
 def relays_of(lon_count):
     tail_from, half_turn = lon_count // 4 - 1, lon_count // 2
-    relays = {dev: [] for dev in (half_turn - 1, lon_count - 1, half_turn)}
-    relays[tail_from], relays[half_turn + tail_from] = [], []
+    first_ones = (half_turn + tail_from, tail_from, half_turn - 1, lon_count - 1, half_turn)
+    relays = {dev: [] for dev in first_ones}
     for first, last in ((tail_from, half_turn - 1), (half_turn + tail_from, lon_count - 1)):
         for dev in range(first + 1, last):
             relays[first if dev <= first + 2 else last].append(dev)
@@ -136,7 +136,9 @@
         load.start()
 
     place = lax.rem(me, half_turn)
-    is_late, is_early, is_mid = place >= half_turn // 2, place == 0, place == tail_from
+    is_late, is_early = place >= half_turn // 2, place == 0
+    in_middle = (lat == lat_count // 2 - 1) | (lat == lat_count // 2)
+    is_mid = (place == tail_from) | (in_middle & jnp.logical_not(is_late | is_early))
     answers = is_late & (lat == lat_count // 2 - 1)
     asks = is_late & (lat == lat_count // 2)
 
@@ -167,7 +169,7 @@
                     barrier, inc=1, device_id=sector(relay), device_id_type=MESH
                 )
 
-    zonal_first = (is_early | is_mid | (me < tail_from)) & (me != 0)
+    zonal_first = jnp.logical_not(is_root)
     peers = 4 - jnp.where(asks, 1, 0) + jnp.where(is_tail, 1, 0) + child_count + jnp.where(is_root, len(relays), 0)
 
     @pl.when(is_root)
@@ -285,11 +287,16 @@
 
         @pl.when(is_root)
         def _():
-            for copy in head_copies:
+            for copy in head_copies[3:]:
                 copy.start()
             head_0_copy.start()
 
     def then_send():
+        @pl.when(is_root)
+        def _():
+            for copy in head_copies[:3]:
+                copy.start()
+
         near[3].start()
 
         @pl.when(jnp.logical_not(asks))
@@ -428,14 +435,15 @@
                 kept = strips[at + r, w, OFF + 8 : OFF + 12, :]
                 state[r, w, OFF + CELLS - SUB : OFF + CELLS, :] = kept
 
-    is_relay = functools.reduce(jnp.logical_or, [me == relay for relay in relays])
+    passing = {relay: copies for relay, copies in passed_on.items() if copies}
+    is_relay = functools.reduce(jnp.logical_or, [me == relay for relay in passing])
 
     def heads_arrived():
         pltpu.make_async_copy(heads.at[2:4], heads.at[2:4], recv_sem.at[8]).wait()
 
     def pass_on():
         with jax.named_scope("pass_on"):
-            for relay, copies in passed_on.items():
+            for relay, copies in passing.items():
 
                 @pl.when(me == relay)
                 def _(copies=copies):
@@ -476,16 +484,17 @@
         for r in range(4):
             for p in range(4):
                 first[r, p, left_row : left_row + SUB, :] = halos[0, 0, r, 4 * p : 4 * p + 4, :]
-        right_strips(0)
-        for r in range(4):
-            fill(4 + r, r, left_start)
-        with jax.named_scope("zonal_strips"):
-            strip_steps(8)
-        right_kept(0)
-        left_kept(4)
-
-        @pl.when(is_tail)
-        def _():
+
+        def edge_strips():
+            right_strips(0)
+            for r in range(4):
+                fill(4 + r, r, left_start)
+
+        def edges_kept():
+            right_kept(0)
+            left_kept(4)
+
+        def far_arrived():
             with jax.named_scope("far_wait"):
 
                 @pl.when(jnp.logical_not(is_relay))
@@ -496,13 +505,43 @@
                 def _():
                     pltpu.make_async_copy(heads.at[0], heads.at[0], recv_sem.at[9]).wait()
 
+        def far_strips(at):
             for n, r in enumerate(FAR):
-                fill(n, r, ends[r])
+                fill(at + n, r, ends[r])
                 for w in range(3):
-                    strips[n, w, OFF + 8 : OFF + 12, :] = heads[r, 4 * w : 4 * w + 4, :]
-                scour[n, 8:12, :] = heads[r, 12:16, :]
+                    strips[at + n, w, OFF + 8 : OFF + 12, :] = heads[r, 4 * w : 4 * w + 4, :]
+                scour[at + n, 8:12, :] = heads[r, 12:16, :]
+
+        def far_kept(at):
+            for n in range(len(FAR)):
+                for w in range(3):
+                    back[n, w, PBASE : PBASE + WIN, :] = strips[at + n, w, OFF : OFF + WIN, :]
+
+        in_one = me == half_turn - 1
+
+        @pl.when(in_one)
+        def _():
+            edge_strips()
+            far_strips(8)
+            with jax.named_scope("zonal_strips"):
+                strip_steps(11)
+            edges_kept()
+            far_kept(8)
+
+        @pl.when(jnp.logical_not(in_one | is_root))
+        def _():
+            edge_strips()
+            with jax.named_scope("zonal_strips"):
+                strip_steps(8)
+            edges_kept()
+
+        @pl.when(is_tail & jnp.logical_not(in_one))
+        def _():
+            far_arrived()
+            far_strips(0)
             with jax.named_scope("far_strips"):
                 strip_steps(3)
+            far_kept(0)
 
         @pl.when(is_root)
         def _():
@@ -525,10 +564,6 @@
                 strip_steps(4)
             left_kept(0)
 
-        for n, r in enumerate(FAR):
-            for w in range(3):
-                back[n, w, PBASE : PBASE + WIN, :] = strips[n, w, OFF : OFF + WIN, :]
-
         for r in range(4):
             change = None
             for w in range(3):
@@ -666,7 +701,7 @@
     def _():
         tail_0_copy.wait_send()
 
-    for relay, copies in passed_on.items():
+    for relay, copies in passing.items():
 
         @pl.when(me == relay)
         def _(copies=copies):

time: 17.2 us -> 17 us (0.988)
  the two profiles are of different devices: /device:TPU:59 before, /device:TPU:121 now
where the time goes in v4:
time: 17 us; the launch traced here: 16.9 us
  Pallas kernels  16.2 us (95%)
  between operations  0.64 us (4%)
    pallas_call x1, Pallas kernels, shards(): pl.pallas_call(functools.partial(kernel, counts), out_shape=(pltpu.VMEM(f...  15.1 us
    pallas_call x1, Pallas kernels, shards(): pl.pallas_call(write_out, out_shape=(pltpu.HBM(flat_shape, F32), pltpu.HB...  1.17 us

profile of v4, /device:TPU:121, one launch (start us, length us, event | category | flops | bytes accessed | tf_op | source)
XLA Modules:
  0.0 16.9 jit_solution(4449141095554485786)
XLA Ops:
  0.6 15.1 %shard_map.94 = (f32[1536,128]{1,0:T(8,128)S(1)}, f32[1536,128]{1,0:T(8,128)S(1)}, f32[16,128]{1,0:T(8,128)S(1)}) custom-call(s32[4]{0:T(128)} %zlen_ref.1, f32[1536,128]{1,0:T(8,128)} %bitcast.8, f32[128,128]{1,0:T(8,128)} %bitcast.10, s32[4,128]{1,0:T(4,128)} %owner_ref.1, f32[1536,128]{1,0:T(8,128)} %bitcast.9, f32[128,128]{1,0:T(8,128)} %bitcast.11, ...), custom_call_target="tpu_custom_call" | custom-call | tf_op jit(solution)/shard_map/pallas_call | solution.py:741
  15.7 1.2 %shard_map.95 = (f32[1536,128]{1,0:T(8,128)}, f32[1536,128]{1,0:T(8,128)}, f32[16,128]{1,0:T(8,128)}) custom-call(f32[1536,128]{1,0:T(8,128)S(1)} %get-tuple-element.9.z, f32[1536,128]{1,0:T(8,128)S(1)} %get-tuple-element.10.m, f32[16,128]{1,0:T(8,128)S(1)} %get-tuple-element.11.c), custom_call_target="tpu_custom_call" | custom-call | tf_op jit(solution)/shard_map/pallas_call | solution.py:791

commit v5 on v4

--- a/solution.py
+++ b/solution.py
@@ -94,6 +94,7 @@
     other_strips,
     scour,
     back,
+    owners,
     edges,
     halos,
     tails,
@@ -517,11 +518,28 @@
                 for w in range(3):
                     back[n, w, PBASE : PBASE + WIN, :] = strips[at + n, w, OFF : OFF + WIN, :]
 
+        def base_parts():
+            for r in range(4):
+                change = None
+                for w in range(3):
+                    value = (
+                        state[r, w, OFF : OFF + CELLS, :] - first[r, w, OFF : OFF + CELLS, :]
+                    )
+                    change = value if change is None else change + value
+                if r in FAR:
+                    change = jnp.where(column < ends[r] - SUB, change, 0.0)
+                    owned = owner[r : r + 1, :].astype(F32)
+                    owners[FAR.index(r), OFF : OFF + CELLS, :] = jnp.broadcast_to(
+                        owned, (LANES, CELLS)
+                    ).T
+                part[r, :, :] = shares(r, change)
+
         in_one = me == half_turn - 1
 
         @pl.when(in_one)
         def _():
             edge_strips()
+            far_arrived()
             far_strips(8)
             with jax.named_scope("zonal_strips"):
                 strip_steps(11)
@@ -534,6 +552,10 @@
             with jax.named_scope("zonal_strips"):
                 strip_steps(8)
             edges_kept()
+
+        @pl.when(jnp.logical_not(is_root))
+        def _():
+            base_parts()
 
         @pl.when(is_tail & jnp.logical_not(in_one))
         def _():
@@ -563,33 +585,50 @@
             with jax.named_scope("far_strips"):
                 strip_steps(4)
             left_kept(0)
-
-        for r in range(4):
-            change = None
+            base_parts()
+
+        @pl.when(is_tail)
+        def _():
+            row = lax.broadcasted_iota(jnp.int32, (8, LANES), 0)
+            for n, r in enumerate(FAR):
+                cell = ends[r] - 8 + row
+                valid = (row >= SUB) & (cell >= 0) & (cell < CELLS)
+                change = None
+                for w in range(3):
+                    value = back[n, w, PBASE : PBASE + 8, :] - first[r, w, pl.ds(ends[r], 8), :]
+                    change = value if change is None else change + value
+                change = jnp.where(valid, change * scale, 0.0)
+                owned = owners[n, pl.ds(ends[r], 8), :]
+                sums = [
+                    jnp.sum(
+                        jnp.where(owned == (me * GLON_DEV - 1 + g).astype(F32), change, 0.0),
+                        axis=0,
+                        keepdims=True,
+                    )
+                    for g in range(GLON_DEV + 2)
+                ]
+                sums.append(jnp.zeros((2, LANES), F32))
+                part[r, :, :] = part[r, :, :] + jnp.concatenate(sums, axis=0)
+
+        @pl.when(jnp.logical_not(is_root))
+        def _():
+            for r in range(4):
+                part[4, r : r + 1, :] = part[r, 0:1, :]
+            back_copy.start()
+
+        @pl.when(jnp.logical_not(is_root | is_last))
+        def _():
+            for r in range(4):
+                part[5, r : r + 1, :] = part[r, 5:6, :]
+            on_copy.start()
+
+        for n, r in enumerate(FAR):
             for w in range(3):
                 value = state[r, w, OFF : OFF + CELLS, :]
                 before = first[r, w, OFF : OFF + CELLS, :]
-                if r in FAR:
-                    n = FAR.index(r)
-                    cut = ends[r]
-                    strip = back[n, w, pl.ds(PBASE + 8 - cut, CELLS), :]
-                    value = jnp.where(column >= cut - SUB, strip, value)
-                    value = jnp.where(column < cut, value, before)
-                    state[r, w, OFF : OFF + CELLS, :] = value
-                change = value - before if change is None else change + (value - before)
-            part[r, :, :] = shares(r, change)
-
-        @pl.when(jnp.logical_not(is_root))
-        def _():
-            for r in range(4):
-                part[4, r : r + 1, :] = part[r, 0:1, :]
-            back_copy.start()
-
-        @pl.when(jnp.logical_not(is_root | is_last))
-        def _():
-            for r in range(4):
-                part[5, r : r + 1, :] = part[r, 5:6, :]
-            on_copy.start()
+                strip = back[n, w, pl.ds(PBASE + 8 - ends[r], CELLS), :]
+                value = jnp.where(column >= ends[r] - SUB, strip, value)
+                state[r, w, OFF : OFF + CELLS, :] = jnp.where(column < ends[r], value, before)
 
     @pl.when(jnp.logical_not(is_early | is_mid))
     def _():
@@ -761,6 +800,7 @@
             pltpu.VMEM((12, 3, SROWS, LANES), F32),
             pltpu.VMEM((12, WIN, LANES), F32),
             pltpu.VMEM((3, 3, PROWS, LANES), F32),
+            pltpu.VMEM((3, ROWS, LANES), F32),
             pltpu.VMEM((2, 2, 4, 16, LANES), F32),
             pltpu.VMEM((2, 2, 4, 16, LANES), F32),
             pltpu.VMEM((4, 16, LANES), F32),

time: 17 us -> 16.7 us (0.982)
  Pallas kernels: 16.2 us -> 16 us
    pallas_call x1, Pallas kernels: 15.1 us -> 14.8 us  [shards(): pl.pallas_call(functools.partial(kernel, counts), out_shape=(pltpu.VMEM(f...]
where the time goes in v5:
time: 16.7 us; the launch traced here: 16.6 us
  Pallas kernels  16 us (96%)
  between operations  0.64 us (4%)
    pallas_call x1, Pallas kernels, shards(): pl.pallas_call(functools.partial(kernel, counts), out_shape=(pltpu.VMEM(f...  14.8 us
    pallas_call x1, Pallas kernels, shards(): pl.pallas_call(write_out, out_shape=(pltpu.HBM(flat_shape, F32), pltpu.HB...  1.17 us

profile of v5, /device:TPU:121, one launch (start us, length us, event | category | flops | bytes accessed | tf_op | source)
XLA Modules:
  0.0 16.6 jit_solution(8011872262438773870)
XLA Ops:
  0.6 14.8 %shard_map.94 = (f32[1536,128]{1,0:T(8,128)S(1)}, f32[1536,128]{1,0:T(8,128)S(1)}, f32[16,128]{1,0:T(8,128)S(1)}) custom-call(s32[4]{0:T(128)} %zlen_ref.1, f32[1536,128]{1,0:T(8,128)} %bitcast.8, f32[128,128]{1,0:T(8,128)} %bitcast.10, s32[4,128]{1,0:T(4,128)} %owner_ref.1, f32[1536,128]{1,0:T(8,128)} %bitcast.9, f32[128,128]{1,0:T(8,128)} %bitcast.11, ...), custom_call_target="tpu_custom_call" | custom-call | tf_op jit(solution)/shard_map/pallas_call | solution.py:780
  15.4 1.2 %shard_map.95 = (f32[1536,128]{1,0:T(8,128)}, f32[1536,128]{1,0:T(8,128)}, f32[16,128]{1,0:T(8,128)}) custom-call(f32[1536,128]{1,0:T(8,128)S(1)} %get-tuple-element.9.z, f32[1536,128]{1,0:T(8,128)S(1)} %get-tuple-element.10.m, f32[16,128]{1,0:T(8,128)S(1)} %get-tuple-element.11.c), custom_call_target="tpu_custom_call" | custom-call | tf_op jit(solution)/shard_map/pallas_call | solution.py:831

commit v6 on v5

--- a/solution.py
+++ b/solution.py
@@ -365,7 +365,11 @@
             )
             return carry
 
-        lax.fori_loop(0, SUB // 2, step, 0)
+        if count <= 4:
+            for t in range(SUB // 2):
+                step(t, 0)
+        else:
+            lax.fori_loop(0, SUB // 2, step, 0)
 
     def fill(n, ch, start):
         for w in range(3):

time: 16.7 us -> 16.6 us (level)
  no operation moved by 1% of the time
where the time goes in v6:
time: 16.6 us; the launch traced here: 16.5 us
  Pallas kernels  15.9 us (96%)
  between operations  0.64 us (4%)
    pallas_call x1, Pallas kernels, shards(): pl.pallas_call(functools.partial(kernel, counts), out_shape=(pltpu.VMEM(f...  14.7 us
    pallas_call x1, Pallas kernels, shards(): pl.pallas_call(write_out, out_shape=(pltpu.HBM(flat_shape, F32), pltpu.HB...  1.17 us

profile of v6, /device:TPU:121, one launch (start us, length us, event | category | flops | bytes accessed | tf_op | source)
XLA Modules:
  0.0 16.5 jit_solution(16138616523960389819)
XLA Ops:
  0.6 14.7 %shard_map.94 = (f32[1536,128]{1,0:T(8,128)S(1)}, f32[1536,128]{1,0:T(8,128)S(1)}, f32[16,128]{1,0:T(8,128)S(1)}) custom-call(s32[4]{0:T(128)} %zlen_ref.1, f32[1536,128]{1,0:T(8,128)} %bitcast.8, f32[128,128]{1,0:T(8,128)} %bitcast.10, s32[4,128]{1,0:T(4,128)} %owner_ref.1, f32[1536,128]{1,0:T(8,128)} %bitcast.9, f32[128,128]{1,0:T(8,128)} %bitcast.11, ...), custom_call_target="tpu_custom_call" | custom-call | tf_op jit(solution)/shard_map/pallas_call | solution.py:784
  15.3 1.2 %shard_map.95 = (f32[1536,128]{1,0:T(8,128)}, f32[1536,128]{1,0:T(8,128)}, f32[16,128]{1,0:T(8,128)}) custom-call(f32[1536,128]{1,0:T(8,128)S(1)} %get-tuple-element.9.z, f32[1536,128]{1,0:T(8,128)S(1)} %get-tuple-element.10.m, f32[16,128]{1,0:T(8,128)S(1)} %get-tuple-element.11.c), custom_call_target="tpu_custom_call" | custom-call | tf_op jit(solution)/shard_map/pallas_call | solution.py:835
